TPU v7x, 32 devices: a whole 2x2x4 slice. The times are simulated.
32 devices in a mesh: dp: 2 (over x), expert: 16 (over z, y, core).
Axes of the slice: x: 2, y: 2, z: 4, core: 2. Of those that a mesh axis runs over, the one named last changes fastest.
Arguments:
- hidden: bfloat16 [2, 1024, 2, 2048], P('dp', 'expert'), may hold values from -6 to 6
- queries: bfloat16 [2, 1024, 2, 4096], P('dp', 'expert'), may hold values from -45 to 45
- latents: bfloat16 [2, 1024, 2, 512], P('dp', 'expert'), may hold values from -165 to 165
- mem_latents: bfloat16 [2, 32, 2, 512], P('dp'), may hold values from -6 to 6
- lengths: int32 [2, 2], P('dp'), may hold values from 512 to 1024
- ids: int32 [2, 1024, 2, 6], P('dp', 'expert'), may hold values from 0 to 15, all different within a row; in each aligned block of 128 rows (0 to 127, 128 to 255, ..., all dimensions but the last counted through in order) at most 50 rows name the same one
- gates: bfloat16 [2, 1024, 2, 6], P('dp', 'expert'), may hold values from 0.049804688 to 0.5
- norm_gain: bfloat16 [2048], replicated, may hold values from 0.25 to 1.75
- w_uv: bfloat16 [8, 512, 128], P('dp'), may hold values from -0.25 to 0.25
- w_out: bfloat16 [1024, 2048], P('dp'), may hold values from -0.1875 to 0.1875
- w_gate: bfloat16 [16, 2048, 704], P('expert'), may hold values from -0.125 to 0.125
- w_up: bfloat16 [16, 2048, 704], P('expert'), may hold values from -0.125 to 0.125
- w_down: bfloat16 [16, 704, 2048], P('expert'), may hold values from -0.21875 to 0.21875
Outputs:
- layer_out: bfloat16 [2, 1024, 2, 2048], P('dp', 'expert')
Inputs may be any that keep to these rules, and one draw needn't show every extreme that they name: `ids`: each row names 6 different experts; the rows of one device (aligned blocks of 128 rows in the order of the leading dimensions) name any one expert at most 50 times, a bound that some block reaches.
All inputs are finite; a program needn't handle non-finite values.
Results may differ from a plain program's by a relative error of at most 0.007.
Values may be sent and summed in bfloat16 or wider, within the bound.
A program may use at most 128 MiB of HBM per device.

v0:
```python
import functools

import jax
import jax.numpy as jnp
from jax import lax
from jax.experimental import pallas as pl
from jax.experimental.pallas import tpu as pltpu
from jax.sharding import PartitionSpec as P

score_scale = 192.0 ** (-0.5)
norm_eps = 1e-06
MESH = pl.DeviceIdType.MESH


def ring_place(n):
    chips = n // 2
    depth = chips // 2
    me = lax.axis_index("expert")
    core = me % 2
    chip = me // 2
    row, col = chip // 2, chip % 2
    pos = col * row + (1 - col) * (chips - 1 - row)

    def device(offset, core_of):
        p = (pos + offset + chips) % chips
        q = p // depth
        r = (1 - q) * p + q * (chips - 1 - p)
        return (2 * r + 1 - q) * 2 + core_of

    return me, core, device


def greet(targets):
    barrier = pltpu.get_barrier_semaphore()
    for target in targets:
        pl.semaphore_signal(barrier, inc=1, device_id={"expert": target}, device_id_type=MESH)
    pl.semaphore_wait(barrier, len(targets))


def remote(src, dst, send_sem, recv_sem, target):
    return pltpu.make_async_remote_copy(
        src_ref=src,
        dst_ref=dst,
        send_sem=send_sem,
        recv_sem=recv_sem,
        device_id={"expert": target},
        device_id_type=MESH,
    )


def gather_kernel(n, cut, x_ref, out_ref, ring_send, ring_recv, pair_send, pair_recv, own_sem):
    chips = n // 2
    half_ring = chips // 2
    rows = x_ref.shape[0]
    last = chips - 2
    me, core, device = ring_place(n)
    partner = device(0, 1 - core)
    ahead = (device(1, core), device(-1, core))
    spans = (pl.ds(0, cut), pl.ds(cut, rows - cut))
    greet((ahead[0], ahead[1], partner))

    def arrival(way, j):
        dist, half = (half_ring, way) if j == last else (j // 2 + 1, j % 2)
        return device(-dist if way == 0 else dist, core), spans[half]

    waits = []
    for way in (0, 1):
        for j in (0, 1):
            if j > last:
                continue
            if j == last and half_ring == 1:
                span = spans[way]
            else:
                span = spans[j]
            copy = remote(
                x_ref.at[span], out_ref.at[me, span],
                ring_send.at[way, j], ring_recv.at[way, j], ahead[way],
            )
            copy.start()
            waits.append(copy)
    share = remote(x_ref, out_ref.at[me], pair_send.at[2 * last + 2], pair_recv.at[2 * last + 2], partner)
    share.start()
    waits.append(share)
    keep = pltpu.make_async_copy(x_ref, out_ref.at[me], own_sem)
    keep.start()

    for j in range(last + 1):
        for way in (0, 1):
            slot, span = arrival(way, j)
            piece = out_ref.at[slot, span]
            remote(piece, piece, ring_send.at[way, j], ring_recv.at[way, j], ahead[way]).wait_recv()
            onward = j + 2
            if j >= last - 2 and j < last:
                onward = last if j == last - 2 + way else None
            if j == last:
                onward = None
            if onward is not None:
                copy = remote(piece, piece, ring_send.at[way, onward], ring_recv.at[way, onward], ahead[way])
                copy.start()
                waits.append(copy)
            index = 2 * j + way
            copy = remote(piece, piece, pair_send.at[index], pair_recv.at[index], partner)
            copy.start()
            waits.append(copy)

    for j in range(last + 1):
        for way in (0, 1):
            dist, half = (half_ring, way) if j == last else (j // 2 + 1, j % 2)
            slot = device(-dist if way == 0 else dist, 1 - core)
            piece = out_ref.at[slot, spans[half]]
            index = 2 * j + way
            remote(piece, piece, pair_send.at[index], pair_recv.at[index], partner).wait_recv()
    other = out_ref.at[partner]
    remote(other, other, pair_send.at[2 * last + 2], pair_recv.at[2 * last + 2], partner).wait_recv()
    for copy in waits:
        copy.wait_send()
    keep.wait()


def ring_gather(x, n, cut, collective_id):
    rows, cols = x.shape
    steps = n // 2 - 1
    return pl.pallas_call(
        functools.partial(gather_kernel, n, cut),
        out_shape=jax.ShapeDtypeStruct((n, rows, cols), x.dtype),
        in_specs=[pl.BlockSpec(memory_space=pltpu.VMEM)],
        out_specs=pl.BlockSpec(memory_space=pl.ANY),
        scratch_shapes=[
            pltpu.SemaphoreType.DMA((2, steps)),
            pltpu.SemaphoreType.DMA((2, steps)),
            pltpu.SemaphoreType.DMA((2 * steps + 1,)),
            pltpu.SemaphoreType.DMA((2 * steps + 1,)),
            pltpu.SemaphoreType.DMA,
        ],
        compiler_params=pltpu.CompilerParams(collective_id=collective_id, has_side_effects=True),
        cost_estimate=pl.CostEstimate(flops=0, bytes_accessed=16 * n * rows * cols, transcendentals=0),
        name="ring_gather_%d" % collective_id,
    )(x)


def reduce_kernel(
    n, rows_ref, mix_ref, out_ref, mine, paired, give, arrived, ring_send, ring_recv, pair_send, pair_recv
):
    chips = n // 2
    half_ring = chips // 2
    half = mine.shape[1] // 2
    last = chips - 2
    me, core, device = ring_place(n)
    partner = device(0, 1 - core)
    ahead = (device(1, core), device(-1, core))
    greet((ahead[0], ahead[1], partner))

    order = [half_ring]
    for k in range(half_ring - 1, 0, -1):
        order += [k, chips - k]
    order.append(0)
    depth = give.shape[0]
    shares, made, seen = {}, [], set()

    def weigh(k, core_of):
        dest = device(k, core_of)
        return jnp.dot(
            mix_ref[dest], rows_ref[dest // 2], preferred_element_type=jnp.float32
        ).astype(mine.dtype)

    def make():
        k = order[len(made)]
        slot = len(made) % depth
        if len(made) >= depth:
            shares[order[len(made) - depth]].wait_send()
        give[slot] = weigh(k, 1 - core)
        shares[k] = remote(give.at[slot], paired.at[k], pair_send.at[k], pair_recv.at[k], partner)
        shares[k].start()
        mine[k] = weigh(k, core)
        made.append(k)

    def bring(k):
        while k not in made or (len(made) < chips and len(made) < order.index(k) + 3):
            make()
        if k not in seen:
            seen.add(k)
            shares[k].wait_recv()

    def index_of(dist, h):
        return 0 if dist == half_ring else 1 + 2 * (half_ring - 1 - dist) + h

    def await_ring(way, j):
        piece = arrived.at[way, j]
        remote(piece, piece, ring_send.at[way, j], ring_recv.at[way, j], ahead[way]).wait_recv()

    sends = []
    for dist in range(half_ring, 0, -1):
        for turn in (0, 1):
            for way in (0, 1):
                if dist == half_ring:
                    if turn == 1:
                        continue
                    h = way
                elif dist == half_ring - 1:
                    h = 1 - way if turn == 0 else way
                else:
                    h = turn
                k = dist if way == 0 else chips - dist
                bring(k)
                span = pl.ds(h * half, half)
                total = mine[k, span].astype(jnp.float32) + paired[k, span].astype(jnp.float32)
                has_prior = dist < half_ring - 1 or (dist == half_ring - 1 and h == way)
                if has_prior:
                    j = index_of(dist + 1, h)
                    await_ring(way, j)
                    total = total + arrived[way, j].astype(jnp.float32)
                mine[k, span] = total.astype(mine.dtype)
                j = index_of(dist, h)
                copy = remote(
                    mine.at[k, span], arrived.at[way, j],
                    ring_send.at[way, j], ring_recv.at[way, j], ahead[way],
                )
                copy.start()
                sends.append(copy)
    bring(0)
    for h in (0, 1):
        span = pl.ds(h * half, half)
        total = mine[0, span].astype(jnp.float32) + paired[0, span].astype(jnp.float32)
        for way in (0, 1):
            j = index_of(1, h)
            await_ring(way, j)
            total = total + arrived[way, j].astype(jnp.float32)
        out_ref[span] = total
    for copy in sends:
        copy.wait_send()
    for k in order[chips - min(depth, chips) :]:
        shares[k].wait_send()


def ring_reduce(rows_in, mix, n, collective_id):
    rows = mix.shape[1]
    cols = rows_in.shape[2]
    chips = n // 2
    dtype = rows_in.dtype
    return pl.pallas_call(
        functools.partial(reduce_kernel, n),
        out_shape=jax.ShapeDtypeStruct((rows, cols), jnp.float32),
        in_specs=[pl.BlockSpec(memory_space=pltpu.VMEM)] * 2,
        out_specs=pl.BlockSpec(memory_space=pltpu.VMEM),
        scratch_shapes=[
            pltpu.VMEM((chips, rows, cols), dtype),
            pltpu.VMEM((chips, rows, cols), dtype),
            pltpu.VMEM((min(4, chips), rows, cols), dtype),
            pltpu.VMEM((2, chips - 1, rows // 2, cols), dtype),
            pltpu.SemaphoreType.DMA((2, chips - 1)),
            pltpu.SemaphoreType.DMA((2, chips - 1)),
            pltpu.SemaphoreType.DMA((chips,)),
            pltpu.SemaphoreType.DMA((chips,)),
        ],
        compiler_params=pltpu.CompilerParams(
            collective_id=collective_id, has_side_effects=True, vmem_limit_bytes=62 * 1024 * 1024
        ),
        cost_estimate=pl.CostEstimate(
            flops=2 * mix.size * cols, bytes_accessed=16 * n * rows * cols, transcendentals=0
        ),
        name="ring_reduce_%d" % collective_id,
    )(rows_in, mix)


def shards(
    hidden,
    queries,
    latents,
    mem_latents,
    lengths,
    ids,
    gates,
    norm_gain,
    w_uv,
    w_out,
    w_gate,
    w_up,
    w_down,
):
    f32, bf16 = jnp.float32, jnp.bfloat16
    local_len, seq_count, model_width = hidden.shape[1:]
    latent_dim = latents.shape[3]
    head_count = queries.shape[3] // latent_dim
    row_count = local_len * seq_count
    n = lax.axis_size("expert")
    dp_size = lax.axis_size("dp")
    me = lax.axis_index("expert")
    core = me % 2
    own_dp = lax.axis_index("dp")
    heads_here, _, value_dim = w_uv.shape
    top_count = ids.shape[3]

    half_heads = heads_here // 2
    uv_half = lax.dynamic_slice_in_dim(w_uv, core * half_heads, half_heads, 0)
    out_half = lax.dynamic_slice_in_dim(
        w_out, core * half_heads * value_dim, half_heads * value_dim, 0
    )
    uv_groups, out_groups, starts = [w_uv], [w_out], [own_dp * heads_here]
    swap = [(i, i ^ 1) for i in range(n)]
    sizes = [heads_here]
    for shift in range(1, dp_size):
        turn = [(i, (i + shift) % dp_size) for i in range(dp_size)]
        source = (own_dp - shift + dp_size) % dp_size
        uv_far = lax.ppermute(uv_half, "dp", turn)
        out_far = lax.ppermute(out_half, "dp", turn)
        uv_near = lax.ppermute(uv_far, "expert", swap)
        out_near = lax.ppermute(out_far, "expert", swap)
        uv_groups += [uv_far, uv_near]
        out_groups += [out_far, out_near]
        starts += [
            source * heads_here + core * half_heads,
            source * heads_here + (1 - core) * half_heads,
        ]
        sizes += [half_heads, half_heads]

    latent_rows = jnp.transpose(latents[0], (1, 0, 2)).reshape(row_count, latent_dim)
    ids_t = jnp.transpose(ids[0], (2, 1, 0)).reshape(top_count, row_count).astype(bf16)
    gates_t = jnp.transpose(gates[0], (2, 1, 0)).reshape(top_count, row_count)
    table = jnp.concatenate([ids_t, gates_t], axis=0).reshape(-1)
    table_rows = -(-table.shape[0] // (16 * latent_dim)) * 16
    table = jnp.pad(table, (0, table_rows * latent_dim - table.shape[0]))
    packed = jnp.concatenate([latent_rows, table.reshape(table_rows, latent_dim)], axis=0)
    all_rows = row_count + table_rows
    cut = (all_rows // 2 + 15) // 16 * 16
    gathered = ring_gather(packed, n, cut, 0)

    segment = gathered[:, :row_count].reshape(n, seq_count, local_len, latent_dim)
    segment = jnp.transpose(segment, (1, 0, 2, 3)).reshape(seq_count, n * local_len, latent_dim)
    memory = jnp.transpose(mem_latents[0], (1, 0, 2))
    mem_count = memory.shape[1]
    keys = jnp.concatenate([memory, segment], axis=1)
    query_rows = jnp.transpose(
        queries[0].reshape(local_len, seq_count, head_count, latent_dim), (1, 2, 0, 3)
    ).reshape(seq_count, head_count * local_len, latent_dim)
    scores = jnp.einsum("sql,sjl->sqj", query_rows, keys, preferred_element_type=f32) * score_scale
    key_pos = lax.broadcasted_iota(jnp.int32, scores.shape, 2) - mem_count
    own_pos = me * local_len + lax.broadcasted_iota(jnp.int32, scores.shape, 1) % local_len
    visible = (key_pos <= own_pos) & (key_pos < lengths[0][:, None, None])
    scores = jnp.where(visible | (key_pos < 0), scores, -jnp.inf)
    weights = jnp.exp(scores - jnp.max(scores, axis=2, keepdims=True))
    total = jnp.sum(weights, axis=2, keepdims=True)
    attended = jnp.einsum("sqj,sjl->sql", weights.astype(bf16), keys, preferred_element_type=f32)
    attended = (attended / total).astype(bf16)
    attended = attended.reshape(seq_count, head_count, local_len, latent_dim)

    attn_out = jnp.zeros((row_count, model_width), f32)
    for uv, out, start, size in zip(uv_groups, out_groups, starts, sizes):
        heads = lax.dynamic_slice_in_dim(attended, start, size, 1)
        values = jnp.einsum("shtl,hlv->sthv", heads, uv, preferred_element_type=f32).astype(bf16)
        attn_out = attn_out + jnp.dot(
            values.reshape(row_count, size * value_dim), out, preferred_element_type=f32
        )

    hidden_rows = jnp.transpose(hidden[0], (1, 0, 2)).reshape(row_count, model_width)
    residual = lax.optimization_barrier(hidden_rows).astype(f32) + attn_out
    mean_square = jnp.mean(residual * residual, axis=-1, keepdims=True)
    normed = (residual * lax.rsqrt(mean_square + norm_eps) * norm_gain.astype(f32)).astype(bf16)

    rows_all = ring_gather(normed, n, row_count // 2, 1)
    experts_here = w_gate.shape[0]
    expert_count = n * experts_here
    capacity = min(row_count, row_count * top_count // expert_count + 2)
    groups = n // 2
    wide = 2 * row_count
    slots = -(-2 * capacity // 16) * 16
    tables = gathered[:, row_count:].reshape(n, -1)[:, : 2 * top_count * row_count]
    tables = tables.reshape(groups, 2, 2, top_count, row_count)
    named = jnp.transpose(tables[:, :, 0], (2, 0, 1, 3)).reshape(top_count, groups, wide)
    scale = jnp.transpose(tables[:, :, 1], (2, 0, 1, 3)).reshape(top_count, groups, wide)
    rows_all = rows_all.reshape(groups, wide, model_width)
    steps = jnp.arange(wide, dtype=jnp.int32)
    earlier = (steps[:, None] < steps[None, :]).astype(bf16)
    made_rows, mixes = [], []
    for e in range(experts_here):
        matches = named == (me * experts_here + e).astype(bf16)
        hit = jnp.any(matches, axis=0)
        gate = jnp.sum(jnp.where(matches, scale.astype(f32), 0.0), axis=0)
        slot = jnp.dot(hit.astype(bf16), earlier, preferred_element_type=f32).astype(jnp.int32)
        slot = jnp.where(hit, slot, -1)
        chosen = slot[:, None, :] == jnp.arange(slots, dtype=jnp.int32)[None, :, None]
        placing = chosen.astype(bf16)
        slot_t = jnp.where(hit, slot, -1).reshape(n, row_count)
        chosen_t = slot_t[:, :, None] == jnp.arange(slots, dtype=jnp.int32)[None, None, :]
        mixes.append(jnp.where(chosen_t, gate.reshape(n, row_count)[:, :, None], 0.0).astype(bf16))
        picked = jnp.einsum("gct,gtd->gcd", placing, rows_all, preferred_element_type=f32)
        picked = picked.astype(bf16).reshape(groups * slots, model_width)
        gate_h = jnp.dot(picked, w_gate[e], preferred_element_type=f32)
        up_h = jnp.dot(picked, w_up[e], preferred_element_type=f32)
        act = (jax.nn.silu(gate_h) * up_h).astype(bf16)
        produced = jnp.dot(act, w_down[e], preferred_element_type=f32).astype(bf16)
        made_rows.append(produced.reshape(groups, slots, model_width))
    made_rows = made_rows[0] if experts_here == 1 else jnp.concatenate(made_rows, axis=1)
    mixing = mixes[0] if experts_here == 1 else jnp.concatenate(mixes, axis=2)
    routed = ring_reduce(made_rows, mixing, n, 2)
    layer_out = (residual + routed).astype(bf16).reshape(seq_count, local_len, model_width)
    return jnp.transpose(layer_out, (1, 0, 2))[None]


def solution(mesh):
    return jax.shard_map(
        shards,
        mesh=mesh,
        in_specs=(
            P("dp", "expert", None, None),
            P("dp", "expert", None, None),
            P("dp", "expert", None, None),
            P("dp", None, None, None),
            P("dp", None),
            P("dp", "expert", None, None),
            P("dp", "expert", None, None),
            P(),
            P("dp", None, None),
            P("dp", None),
            P("expert", None, None),
            P("expert", None, None),
            P("expert", None, None),
        ),
        out_specs=P("dp", "expert", None, None),
        check_vma=False,
    )
```

profile of v0, /device:TPU:0, one launch (start us, length us, event | category | flops | bytes accessed | tf_op | source)
XLA Modules:
  0.0 180.4 jit_solution(15198277275547799506)
XLA Ops:
  0.0 1.0 copy-done
  1.1 3.0 %collective-permute-start = (bf16[2,512,128]{2,1,0:T(8,128)(2,1)S(1)}, bf16[2,512,128]{2,1,0:T(8,128)(2,1)}, u32[]{:S(2)}, u32[]{:S(2)}) collective-permute-start(bf16[2,512,128]{2,1,0:T(8,128)(2,1)S(1)} %constant_dynamic-slice_fusion.3), channel_id=1, source_target_pairs={{0,16},{16,0},{1,17},{17,1},{2,18},{18,2},{3,19},{19,3},{4,20},{20... | collective-permute-start | bytes 786440 | tf_op jit(solution)/shard_map/ppermute | solution.py:304
  4.1 2.3 %constant_dynamic-slice_fusion.1 = bf16[256,2048]{1,0:T(8,128)(2,1)} fusion(bf16[512,2048]{1,0:T(8,128)(2,1)} %param.22, s32[]{:T(128)S(6)} %select_n.59), kind=kLoop, calls=%fused_computation.75 | loop fusion | bytes 2097156 | tf_op jit(solution)/shard_map/dynamic_slice | solution.py:295
  8.3 23.6 %ring_gather_0.1 = bf16[16,144,512]{2,1,0:T(8,128)(2,1)} custom-call(bf16[144,512]{1,0:T(8,128)(2,1)} %pad_maximum_fusion.5.x_ref), custom_call_target="tpu_custom_call" | custom-call | bytes 18874368 | tf_op jit(solution)/shard_map/ring_gather_0/pallas_call | solution.py:123
  32.0 1.6 slice-done
  33.6 1.5 copy.53
  35.1 1.8 reshape_squeeze.3
  37.5 3.7 %fusion.49 = (f32[2,512]{1,0:T(2,128)S(1)}, f32[2,512,1056]{1,2,0:T(8,128)S(1)}) fusion(bf16[2,512,512]{2,1,0:T(8,128)(2,1)S(1)} %bitcast.144, bf16[2,1024,512]{2,1,0:T(8,128)(2,1)} %bitcast.141, bf16[2,32,512]{2,1,0:T(8,128)(2,1)S(1)} %bitcast.154, pred[1056]{0:T(1024)(128)(4,1)S(1)} %broadcast_compare_fusion, s32[2]{0:T(128)S(1)} %bitcast.159, ...), kind=kOutput, calls=%fused_computation.83 | convolution fusion | flops 1121352704 | bytes 7550636 | tf_op jit(solution)/shard_map/sql,sjl->sqj/dot_general | solution.py:335
  41.9 1.0 copy-done.2
  42.9 1.7 divide_convert_fusion
  44.6 1.0 copy-done.3
  46.4 2.1 %fusion.30 = f32[128,2048]{1,0:T(8,128)S(1)} fusion(bf16[512,2048]{1,0:T(8,128)(2,1)} %param.22, bf16[16,8,4,128]{3,2,1,0:T(4,128)(2,1)S(1)} %bitcast.145), kind=kOutput, calls=%fused_computation.47 | convolution fusion | flops 268435456 | bytes 3276800 | tf_op jit(solution)/shard_map/dot_general | solution.py:350
  49.0 1.4 select_convert_fusion.mix_ref
  50.5 1.1 constant_dynamic-slice_fusion
  51.6 1.2 copy.50
  52.8 1.2 fusion.16
  56.1 46.9 %ring_gather_1.1 = bf16[16,128,2048]{2,1,0:T(8,128)(2,1)} custom-call(bf16[128,2048]{1,0:T(8,128)(2,1)} %multiply_convert_fusion.1.x_ref), custom_call_target="tpu_custom_call" | custom-call | bytes 67108864 | tf_op jit(solution)/shard_map/ring_gather_1/pallas_call | solution.py:123
  103.0 4.8 %convolution_convert_fusion.1 = bf16[8,112,2048]{2,1,0:T(8,128)(2,1)S(1)} fusion(bf16[8,256,2048]{2,1,0:T(8,128)(2,1)} %bitcast.133, s32[8,256]{1,0:T(8,128)S(1)} %get-tuple-element.12), kind=kOutput, calls=%fused_computation.9 | convolution fusion | flops 941588480 | bytes 12066816 | tf_op jit(solution)/shard_map/gct,gtd->gcd/dot_general | solution.py:385
  107.8 1.8 %copy-done.1 = bf16[8,112,2048]{2,1,0:T(8,128)(2,1)} copy-done((bf16[8,112,2048]{2,1,0:T(8,128)(2,1)}, bf16[8,112,2048]{2,1,0:T(8,128)(2,1)S(1)}, u32[]{:S(2)}) %copy-start.1) | copy-done | bytes 3670040
  109.6 4.7 %fusion.5 = f32[896,704]{0,1:T(8,128)} fusion(bf16[896,2048]{1,0:T(8,128)(2,1)S(1)} %bitcast.136, bf16[1,2048,704]{1,2,0:T(8,128)(2,1)S(1)} %copy-done.8), kind=kOutput, calls=%fused_computation.11 | convolution fusion | flops 2583691264 | bytes 9076736 | tf_op jit(solution)/shard_map/dot_general | solution.py:388
  114.4 12.4 %convolution_convert_fusion = bf16[896,2048]{1,0:T(8,128)(2,1)} fusion(bf16[1,704,2048]{2,1,0:T(8,128)(2,1)} %param.25, f32[896,704]{0,1:T(8,128)} %fusion.5, bf16[896,2048]{1,0:T(8,128)(2,1)} %bitcast.137, bf16[1,2048,704]{1,2,0:T(8,128)(2,1)} %param.23), kind=kOutput, calls=%fused_computation.8 | convolution fusion | flops 5173002240 | bytes 15630336 | tf_op jit(solution)/shard_map/dot_general | solution.py:390
  126.7 51.0 %ring_reduce_2.1 = f32[128,2048]{1,0:T(8,128)} custom-call(bf16[8,112,2048]{2,1,0:T(8,128)(2,1)} %bitcast.139, bf16[16,128,112]{2,1,0:T(8,128)(2,1)} %select_convert_fusion.mix_ref), custom_call_target="tpu_custom_call" | custom-call | flops 939524096 | bytes 67108864 | tf_op jit(solution)/shard_map/ring_reduce_2/pallas_call | solution.py:240
  177.7 1.3 add_convert_fusion
  179.1 1.3 copy.104
  (59 shorter events, 6.6 us)
Async XLA Ops:
  0.0 1.0 copy-start
  0.0 7.4 %copy-start.5 = (s32[1,64,2,6]{1,2,3,0:T(2,128)S(1)}, s32[1,64,2,6]{1,2,3,0:T(2,128)}, u32[]{:S(2)}) copy-start(s32[1,64,2,6]{1,2,3,0:T(2,128)} %param.18) | copy-start | bytes 9220
  0.0 7.5 %copy-start.7 = (bf16[1,64,2,6]{1,2,3,0:T(2,128)(2,1)S(1)}, bf16[1,64,2,6]{1,2,3,0:T(2,128)(2,1)}, u32[]{:S(2)}) copy-start(bf16[1,64,2,6]{1,2,3,0:T(2,128)(2,1)} %param.19) | copy-start | bytes 4612
  1.1 49.4 %collective-permute-start = (bf16[2,512,128]{2,1,0:T(8,128)(2,1)S(1)}, bf16[2,512,128]{2,1,0:T(8,128)(2,1)}, u32[]{:S(2)}, u32[]{:S(2)}) collective-permute-start(bf16[2,512,128]{2,1,0:T(8,128)(2,1)S(1)} %constant_dynamic-slice_fusion.3), channel_id=1, source_target_pairs={{0,16},{16,0},{1,17},{17,1},{2,18},{18,2},{3,19},{19,3},{4,20},{20... | collective-permute-start | bytes 786440 | tf_op jit(solution)/shard_map/ppermute | solution.py:304
  6.4 42.1 %collective-permute-start.1 = (bf16[256,2048]{1,0:T(8,128)(2,1)}, bf16[256,2048]{1,0:T(8,128)(2,1)S(1)}, u32[]{:S(2)}, u32[]{:S(2)}) collective-permute-start(bf16[256,2048]{1,0:T(8,128)(2,1)} %constant_dynamic-slice_fusion.1), channel_id=1, source_target_pairs={{0,16},{16,0},{1,17},{17,1},{2,18},{18,2},{3,19},{19,3},{4,20},{20... | collective-permute-start | bytes 3145736 | tf_op jit(solution)/shard_map/ppermute | solution.py:305
  32.0 1.6 slice-start
  32.0 3.1 %copy-start.4 = (bf16[1,32,2,512]{3,2,1,0:T(2,128)(2,1)S(1)}, bf16[1,32,2,512]{3,2,1,0:T(2,128)(2,1)}, u32[]{:S(2)}) copy-start(bf16[1,32,2,512]{3,2,1,0:T(2,128)(2,1)} %param.16) | copy-start | bytes 196612
  35.1 2.4 %copy-start.9 = (s32[1,2]{1,0:T(1,128)S(1)}, s32[1,2]{1,0:T(1,128)}, u32[]{:S(2)}) copy-start(s32[1,2]{1,0:T(1,128)} %param.17) | copy-start | bytes 28
  41.3 1.6 copy-start.2
  42.9 3.1 %slice-start.1 = ((bf16[16,144,512]{2,1,0:T(8,128)(2,1)}), bf16[16,16,512]{2,1,0:T(8,128)(2,1)S(1)}, s32[]{:S(2)}) async-start(bf16[16,144,512]{2,1,0:T(8,128)(2,1)} %ring_gather_0.1), calls=%async_computation.1 | async-start | bytes 524288 | tf_op jit(solution)/shard_map/slice | solution.py:366
  44.6 1.0 copy-start.3
  46.4 6.4 %copy-start.6 = (bf16[2048]{0:T(1024)(128)(2,1)S(1)}, bf16[2048]{0:T(1024)(128)(2,1)}, u32[]{:S(2)}) copy-start(bf16[2048]{0:T(1024)(128)(2,1)} %param.20) | copy-start | bytes 12292
  48.6 6.1 %collective-permute-start.3 = (bf16[256,2048]{1,0:T(8,128)(2,1)S(1)}, bf16[256,2048]{1,0:T(8,128)(2,1)S(1)}, u32[]{:S(2)}, u32[]{:S(2)}) collective-permute-start(bf16[256,2048]{1,0:T(8,128)(2,1)S(1)} %collective-permute-done.1), channel_id=1, source_target_pairs={{0,1},{1,0},{2,3},{3,2},{4,5},{5,4},{6,7},{7,6},{8,9},{9,8},{10,11... | collective-permute-start | bytes 3145736 | tf_op jit(solution)/shard_map/ppermute | solution.py:307
  50.4 3.7 %collective-permute-start.2 = (bf16[2,512,128]{2,1,0:T(8,128)(2,1)}, bf16[2,512,128]{2,1,0:T(8,128)(2,1)S(1)}, u32[]{:S(2)}, u32[]{:S(2)}) collective-permute-start(bf16[2,512,128]{2,1,0:T(8,128)(2,1)} %collective-permute-done), channel_id=1, source_target_pairs={{0,1},{1,0},{2,3},{3,2},{4,5},{5,4},{6,7},{7,6},{8,9},{9,8},{10,11... | collective-permute-start | bytes 786440 | tf_op jit(solution)/shard_map/ppermute | solution.py:306
  103.0 6.6 %copy-start.8 = (bf16[1,2048,704]{1,2,0:T(8,128)(2,1)S(1)}, bf16[1,2048,704]{1,2,0:T(8,128)(2,1)}, u32[]{:S(2)}) copy-start(bf16[1,2048,704]{1,2,0:T(8,128)(2,1)} %param.24) | copy-start | bytes 8650756
  107.8 1.8 %copy-start.1 = (bf16[8,112,2048]{2,1,0:T(8,128)(2,1)}, bf16[8,112,2048]{2,1,0:T(8,128)(2,1)S(1)}, u32[]{:S(2)}) copy-start(bf16[8,112,2048]{2,1,0:T(8,128)(2,1)S(1)} %convolution_convert_fusion.1) | copy-start | bytes 11010052
where the time goes:
time: 181 us; the launch traced here: 180 us
  Pallas kernels  121 us (67%)
  matrix products  31.9 us (18%)
  local copies, waits for them, and re-layouts  17.9 us (10%)
  other arithmetic  5.07 us (3%)
  starting transfers between devices  3.64 us (2%)
    pallas_call x2, Pallas kernels, ring_gather(): pl.pallas_call(functools.partial(gather_kernel, n, cut), out_shape=jax.Sh...  70.5 us
    pallas_call x1, Pallas kernels, ring_reduce(): pl.pallas_call(functools.partial(reduce_kernel, n), out_shape=jax.ShapeDt...  51 us
    dot_general x1, matrix products, shards(): produced = jnp.dot(act, w_down[e], preferred_element_type=f32).astype(bf16)  12.4 us
    unnamed x22, local copies, waits for them, and re-layouts  5 us
    dot_general x1, matrix products, shards(): jnp.einsum('gct,gtd->gcd', placing, rows_all, preferred_element_type=f32)  4.79 us
    dot_general x1, matrix products, shards(): up_h = jnp.dot(picked, w_up[e], preferred_element_type=f32)  4.72 us
    dot_general x1, matrix products, shards(): jnp.einsum('sql,sjl->sqj', query_rows, keys, preferred_element_type=f32)  3.72 us
  transfers between devices with their start and end apart: 4, of which 0 were waited for; matrix products, arithmetic and copies ran while one was open for 12% of the time, Pallas kernels for 13%

commit v1 on v0

--- a/solution.py
+++ b/solution.py
@@ -262,6 +262,209 @@
     )(rows_in, mix)
 
 
+def expert_kernel(
+    n, x_ref, keep_ref, place_ref, mix_ref, gate_hbm, up_hbm, down_hbm, out_ref,
+    rows, w_gate, w_up, w_down, act, mine, paired, give, arrived,
+    load_sem, gather_send, gather_recv, swap_send, swap_recv, ring_send, ring_recv, pair_send, pair_recv,
+):
+    f32 = jnp.float32
+    chips = n // 2
+    half_ring = chips // 2
+    count, width = x_ref.shape
+    half = count // 2
+    slots = place_ref.shape[1]
+    last = chips - 2
+    me, core, device = ring_place(n)
+    partner = device(0, 1 - core)
+    ahead = (device(1, core), device(-1, core))
+    spans = (pl.ds(0, half), pl.ds(half, half))
+    loads = [
+        pltpu.make_async_copy(src, dst, load_sem.at[i])
+        for i, (src, dst) in enumerate(((gate_hbm, w_gate), (up_hbm, w_up), (down_hbm, w_down)))
+    ]
+    for load in loads:
+        load.start()
+    greet((ahead[0], ahead[1], partner))
+    waits = []
+
+    def send(copy):
+        copy.start()
+        waits.append(copy)
+
+    def step_of(way, j):
+        return (half_ring, way) if j == last else (j // 2 + 1, j % 2)
+
+    def offset(way, dist):
+        return dist if way == 0 else chips - dist
+
+    for j in (0, 1):
+        for way in (0, 1):
+            send(remote(
+                x_ref.at[spans[j]], rows.at[me, spans[j]],
+                gather_send.at[way, j], gather_recv.at[way, j], ahead[way],
+            ))
+    send(remote(x_ref, rows.at[me], swap_send.at[2 * last + 2], swap_recv.at[2 * last + 2], partner))
+    rows[me] = x_ref[...]
+
+    def start_experts(ks):
+        picked = []
+        for k in ks:
+            first = device(k, 0)
+            held = rows[pl.ds(first, 2)].reshape(2 * count, width)
+            picked.append(jnp.dot(place_ref[first // 2], held, preferred_element_type=f32).astype(jnp.bfloat16))
+        picked = picked[0] if len(ks) == 1 else jnp.concatenate(picked, axis=0)
+        along = (((1,), (1,)), ((), ()))
+        gate_h = lax.dot_general(picked, w_gate[...], along, preferred_element_type=f32)
+        up_h = lax.dot_general(picked, w_up[...], along, preferred_element_type=f32)
+        act[pl.ds(0, len(ks) * slots)] = (gate_h / (1.0 + jnp.exp(-gate_h)) * up_h).astype(jnp.bfloat16)
+
+    shares = {}
+
+    def end_experts(ks):
+        made = jnp.dot(act[pl.ds(0, len(ks) * slots)], w_down[...], preferred_element_type=f32).astype(jnp.bfloat16)
+        for i, k in enumerate(ks):
+            part = made[i * slots : (i + 1) * slots]
+            give[k] = jnp.dot(mix_ref[device(k, 1 - core)], part, preferred_element_type=f32).astype(give.dtype)
+            shares[k] = remote(give.at[k], paired.at[k], pair_send.at[k], pair_recv.at[k], partner)
+            send(shares[k])
+            mine[k] = jnp.dot(mix_ref[device(k, core)], part, preferred_element_type=f32).astype(mine.dtype)
+
+    seen = set()
+
+    def bring(k):
+        if k not in seen:
+            seen.add(k)
+            shares[k].wait_recv()
+
+    def index_of(dist, h):
+        return 0 if dist == half_ring else 1 + 2 * (half_ring - 1 - dist) + h
+
+    def await_ring(way, j):
+        piece = arrived.at[way, j]
+        remote(piece, piece, ring_send.at[way, j], ring_recv.at[way, j], ahead[way]).wait_recv()
+
+    def advance(dist, chain):
+        for way in (0, 1):
+            h = way if chain == 0 else 1 - way
+            k = offset(way, dist)
+            bring(k)
+            total = mine[k, spans[h]].astype(f32) + paired[k, spans[h]].astype(f32)
+            if dist < half_ring - chain:
+                j = index_of(dist + 1, h)
+                await_ring(way, j)
+                total = total + arrived[way, j].astype(f32)
+            mine[k, spans[h]] = total.astype(mine.dtype)
+            j = index_of(dist, h)
+            send(remote(
+                mine.at[k, spans[h]], arrived.at[way, j],
+                ring_send.at[way, j], ring_recv.at[way, j], ahead[way],
+            ))
+
+    other = rows.at[partner]
+    remote(other, other, swap_send.at[2 * last + 2], swap_recv.at[2 * last + 2], partner).wait_recv()
+    for load in loads:
+        load.wait()
+    start_experts([0])
+    end_experts([0])
+
+    tasks = []
+    for j in range(last + 1):
+        for way in (0, 1):
+            dist, h = step_of(way, j)
+            piece = rows.at[device(-dist if way == 0 else dist, core), spans[h]]
+            remote(piece, piece, gather_send.at[way, j], gather_recv.at[way, j], ahead[way]).wait_recv()
+            onward = j + 2
+            if last - 2 <= j < last:
+                onward = last if j == last - 2 + way else None
+            if j == last:
+                onward = None
+            if onward is not None:
+                send(remote(
+                    piece, piece, gather_send.at[way, onward], gather_recv.at[way, onward], ahead[way]
+                ))
+            send(remote(piece, piece, swap_send.at[2 * j + way], swap_recv.at[2 * j + way], partner))
+        if j % 2 == 1 or j == last:
+            for i in ((j - 1, j) if j % 2 == 1 else (j,)):
+                for way in (0, 1):
+                    dist, h = step_of(way, i)
+                    piece = rows.at[device(-dist if way == 0 else dist, 1 - core), spans[h]]
+                    remote(piece, piece, swap_send.at[2 * i + way], swap_recv.at[2 * i + way], partner).wait_recv()
+            dist = step_of(0, j)[0]
+            ks = [half_ring] if j == last else [dist, chips - dist]
+            tasks += [functools.partial(start_experts, ks), functools.partial(end_experts, ks)]
+        for _ in range(min(len(tasks), 1 if j < last - 1 else len(tasks))):
+            tasks.pop(0)()
+        if j == last - 1:
+            advance(half_ring - 1, 1)
+
+    advance(half_ring, 0)
+    for dist in range(half_ring - 2, 0, -1):
+        advance(dist, 1)
+        advance(dist + 1, 0)
+    advance(1, 0)
+
+    bring(0)
+    for h in (0, 1):
+        total = mine[0, spans[h]].astype(f32) + paired[0, spans[h]].astype(f32)
+        for way in (0, 1):
+            j = index_of(1, h)
+            await_ring(way, j)
+            total = total + arrived[way, j].astype(f32)
+        out_ref[spans[h]] = (keep_ref[spans[h]] + total).astype(out_ref.dtype)
+    for copy in waits:
+        copy.wait_send()
+
+
+def expert_bytes(n, count, width, inner, slots):
+    chips = n // 2
+    held = n * count * width + 3 * width * inner + 3 * chips * count * width + (chips - 1) * count * width
+    held += 6 * count * width + 2 * chips * slots * 2 * count
+    return 2 * held + 4 * 2 * slots * (2 * inner + 2 * width)
+
+
+def ring_experts(x, keep, place, mix, w_gate_t, w_up_t, w_down, n, collective_id):
+    count, width = x.shape
+    chips = n // 2
+    steps = chips - 1
+    inner = w_down.shape[0]
+    slots = place.shape[1]
+    dtype = x.dtype
+    dma = pltpu.SemaphoreType.DMA
+    return pl.pallas_call(
+        functools.partial(expert_kernel, n),
+        out_shape=jax.ShapeDtypeStruct((count, width), dtype),
+        in_specs=[pl.BlockSpec(memory_space=pltpu.VMEM)] * 4 + [pl.BlockSpec(memory_space=pl.ANY)] * 3,
+        out_specs=pl.BlockSpec(memory_space=pltpu.VMEM),
+        scratch_shapes=[
+            pltpu.VMEM((n, count, width), dtype),
+            pltpu.VMEM((inner, width), dtype),
+            pltpu.VMEM((inner, width), dtype),
+            pltpu.VMEM((inner, width), dtype),
+            pltpu.VMEM((2 * slots, inner), dtype),
+            pltpu.VMEM((chips, count, width), dtype),
+            pltpu.VMEM((chips, count, width), dtype),
+            pltpu.VMEM((chips, count, width), dtype),
+            pltpu.VMEM((2, steps, count // 2, width), dtype),
+            dma((3,)),
+            dma((2, steps)),
+            dma((2, steps)),
+            dma((2 * steps + 1,)),
+            dma((2 * steps + 1,)),
+            dma((2, steps)),
+            dma((2, steps)),
+            dma((chips,)),
+            dma((chips,)),
+        ],
+        compiler_params=pltpu.CompilerParams(
+            collective_id=collective_id, has_side_effects=True, vmem_limit_bytes=62 * 1024 * 1024
+        ),
+        cost_estimate=pl.CostEstimate(
+            flops=6 * chips * slots * width * inner, bytes_accessed=32 * n * count * width, transcendentals=0
+        ),
+        name="ring_experts_%d" % collective_id,
+    )(x, keep, place, mix, w_gate_t, w_up_t, w_down)
+
+
 def shards(
     hidden,
     queries,
@@ -356,18 +559,27 @@
     mean_square = jnp.mean(residual * residual, axis=-1, keepdims=True)
     normed = (residual * lax.rsqrt(mean_square + norm_eps) * norm_gain.astype(f32)).astype(bf16)
 
-    rows_all = ring_gather(normed, n, row_count // 2, 1)
     experts_here = w_gate.shape[0]
     expert_count = n * experts_here
     capacity = min(row_count, row_count * top_count // expert_count + 2)
     groups = n // 2
     wide = 2 * row_count
-    slots = -(-2 * capacity // 16) * 16
+    slots = -(-2 * capacity // 128) * 128
+    inner = w_down.shape[1]
+    joined = (
+        experts_here == 1
+        and groups >= 4
+        and row_count % 32 == 0
+        and expert_bytes(n, row_count, model_width, inner, slots) < 52 * 1024 * 1024
+    )
+    if not joined:
+        slots = -(-2 * capacity // 16) * 16
     tables = gathered[:, row_count:].reshape(n, -1)[:, : 2 * top_count * row_count]
     tables = tables.reshape(groups, 2, 2, top_count, row_count)
     named = jnp.transpose(tables[:, :, 0], (2, 0, 1, 3)).reshape(top_count, groups, wide)
     scale = jnp.transpose(tables[:, :, 1], (2, 0, 1, 3)).reshape(top_count, groups, wide)
-    rows_all = rows_all.reshape(groups, wide, model_width)
+    if not joined:
+        rows_all = ring_gather(normed, n, row_count // 2, 1).reshape(groups, wide, model_width)
     steps = jnp.arange(wide, dtype=jnp.int32)
     earlier = (steps[:, None] < steps[None, :]).astype(bf16)
     made_rows, mixes = [], []
@@ -382,6 +594,12 @@
         slot_t = jnp.where(hit, slot, -1).reshape(n, row_count)
         chosen_t = slot_t[:, :, None] == jnp.arange(slots, dtype=jnp.int32)[None, None, :]
         mixes.append(jnp.where(chosen_t, gate.reshape(n, row_count)[:, :, None], 0.0).astype(bf16))
+        if joined:
+            layer_out = ring_experts(
+                normed, residual, placing, mixes[0],
+                jnp.transpose(w_gate[0]), jnp.transpose(w_up[0]), w_down[0], n, 3,
+            )
+            return jnp.transpose(layer_out.reshape(seq_count, local_len, model_width), (1, 0, 2))[None]
         picked = jnp.einsum("gct,gtd->gcd", placing, rows_all, preferred_element_type=f32)
         picked = picked.astype(bf16).reshape(groups * slots, model_width)
         gate_h = jnp.dot(picked, w_gate[e], preferred_element_type=f32)

time: 181 us -> 149 us (0.82)
  matrix products: 31.9 us -> 10 us
  Pallas kernels: 121 us -> 114 us
  local copies, waits for them, and re-layouts: 17.9 us -> 16 us
    pallas_call x2 -> x1, Pallas kernels: 70.5 us -> 23.6 us  [ring_gather(): pl.pallas_call(functools.partial(gather_kernel, n, cut), out_shape=jax.Sh...]
    pallas_call x1, Pallas kernels: 51 us -> 90.1 us  [ring_experts(): pl.pallas_call(functools.partial(expert_kernel, n), out_shape=jax.ShapeDt...]
    dot_general x3 -> x0, matrix products: 21.9 us -> none  [the longest x1 12.4 us: shards(): produced = jnp.dot(act, w_down[e], preferred_element_type=f32).astype(bf16)]
    unnamed x22 -> x24, local copies, waits for them, and re-layouts: 5 us -> 1.9 us
    ppermute x1, starting transfers between devices: 0.03 us -> 2.97 us  [shards(): out_far = lax.ppermute(out_half, 'dp', turn)]
    ppermute x1, starting transfers between devices: 3.03 us -> 0.1 us  [shards(): uv_far = lax.ppermute(uv_half, 'dp', turn)]
  transfers between devices with their start and end apart: 4 -> 4, of which waited for: 0 -> 0; matrix products, arithmetic and copies ran while one was open for 12% -> 14% of each run, Pallas kernels for 13% -> 16%
where the time goes in v1:
time: 149 us
  Pallas kernels  114 us (77%)
  local copies, waits for them, and re-layouts  16 us (11%)
  matrix products  10 us (7%)
  other arithmetic  4.87 us (3%)
  starting transfers between devices  3.58 us (2%)
    pallas_call x1, Pallas kernels, ring_experts(): pl.pallas_call(functools.partial(expert_kernel, n), out_shape=jax.ShapeDt...  90.1 us
    pallas_call x1, Pallas kernels, ring_gather(): pl.pallas_call(functools.partial(gather_kernel, n, cut), out_shape=jax.Sh...  23.6 us
    dot_general x1, matrix products, shards(): jnp.einsum('sql,sjl->sqj', query_rows, keys, preferred_element_type=f32)  3.72 us
  transfers between devices with their start and end apart: 4, of which 0 were waited for; matrix products, arithmetic and copies ran while one was open for 14% of the time, Pallas kernels for 16%

profile of v1, /device:TPU:0, one launch (start us, length us, event | category | flops | bytes accessed | tf_op | source)
XLA Modules:
  0.0 148.5 jit_solution(3429242529362579953)
XLA Ops:
  0.0 2.4 %constant_dynamic-slice_fusion.1 = bf16[256,2048]{1,0:T(8,128)(2,1)} fusion(bf16[512,2048]{1,0:T(8,128)(2,1)} %param.22, s32[]{:T(128)S(6)} %select_n.59), kind=kLoop, calls=%fused_computation.66 | loop fusion | bytes 2097156 | tf_op jit(solution)/shard_map/dynamic_slice | solution.py:498
  2.4 3.0 %collective-permute-start.1 = (bf16[256,2048]{1,0:T(8,128)(2,1)}, bf16[256,2048]{1,0:T(8,128)(2,1)S(1)}, u32[]{:S(2)}, u32[]{:S(2)}) collective-permute-start(bf16[256,2048]{1,0:T(8,128)(2,1)} %constant_dynamic-slice_fusion.1), channel_id=1, source_target_pairs={{0,16},{16,0},{1,17},{17,1},{2,18},{18,2},{3,19},{19,3},{4,20},{20... | collective-permute-start | bytes 3145736 | tf_op jit(solution)/shard_map/ppermute | solution.py:508
  5.5 1.8 %reshape_squeeze.3 = bf16[64,2,8,512]{3,2,1,0:T(8,128)(2,1)S(1)} reshape(bf16[1,64,2,4096]{3,2,1,0:T(2,128)(2,1)} %param.14) | data formatting | bytes 2097152 | tf_op jit(solution)/shard_map/reshape;squeeze | solution.py:536
  7.3 1.6 %copy.54 = bf16[2,8,64,512]{3,2,1,0:T(8,128)(2,1)} copy(bf16[2,8,64,512]{3,1,0,2:T(8,128)(2,1)S(1)} %bitcast.123) | data formatting | bytes 2097152 | tf_op jit(solution)/shard_map/transpose | solution.py:535
  9.2 0.7 pad_maximum_fusion.5.x_ref
  9.8 23.6 %ring_gather_0.1 = bf16[16,144,512]{2,1,0:T(8,128)(2,1)} custom-call(bf16[144,512]{1,0:T(8,128)(2,1)} %pad_maximum_fusion.5.x_ref), custom_call_target="tpu_custom_call" | custom-call | bytes 18874368 | tf_op jit(solution)/shard_map/ring_gather_0/pallas_call | solution.py:123
  33.5 1.5 %slice-done = bf16[16,128,512]{2,1,0:T(8,128)(2,1)S(1)} async-done(((bf16[16,144,512]{2,1,0:T(8,128)(2,1)}), bf16[16,128,512]{2,1,0:T(8,128)(2,1)S(1)}, s32[]{:S(2)}) %slice-start) | async-done | bytes 2097176 | tf_op jit(solution)/shard_map/slice | solution.py:530
  35.1 1.5 %copy.53 = bf16[2,16,64,512]{3,2,1,0:T(8,128)(2,1)} copy(bf16[2,16,64,512]{3,2,0,1:T(8,128)(2,1)S(1)} %bitcast.121) | data formatting | bytes 4194304 | tf_op jit(solution)/shard_map/transpose | solution.py:531
  36.7 3.7 %fusion.39 = (f32[2,512]{1,0:T(2,128)S(1)}, f32[2,512,1056]{1,2,0:T(8,128)S(1)}) fusion(bf16[2,512,512]{2,1,0:T(8,128)(2,1)S(1)} %bitcast.127, bf16[2,1024,512]{2,1,0:T(8,128)(2,1)} %bitcast.124, bf16[2,32,512]{2,1,0:T(8,128)(2,1)S(1)} %bitcast.138, pred[1056]{0:T(1024)(128)(4,1)S(1)} %broadcast_compare_fusion, s32[2]{0:T(128)S(1)} %bitcast.146, ...), kind=kOutput, calls=%fused_computation.73 | convolution fusion | flops 1121352704 | bytes 7550636 | tf_op jit(solution)/shard_map/sql,sjl->sqj/dot_general | solution.py:538
  40.4 0.6 fusion.2
  41.0 1.0 copy-done.2
  42.0 1.7 %divide_convert_fusion = bf16[2,512,512]{2,1,0:T(8,128)(2,1)S(1)} fusion(f32[2,512]{1,0:T(2,128)S(1)} %fusion.2, bf16[2,1024,512]{2,1,0:T(8,128)(2,1)S(1)} %bitcast.125, bf16[2,32,512]{2,1,0:T(8,128)(2,1)S(1)} %bitcast.139, f32[2,512,1056]{1,2,0:T(8,128)S(1)} %get-tuple-element.8, f32[2,512]{1,0:T(2,128)S(1)} %get-tuple-element.7), kind=kOutput, calls=%fused_computation.14 | convolution fusion | flops 1114832896 | bytes 7544832 | tf_op jit(solution)/shard_map/sqj,sjl->sql/dot_general | solution.py:545
  44.0 0.7 copy-done.4
  45.3 2.0 %fusion.21 = f32[128,2048]{1,0:T(8,128)S(1)} fusion(bf16[512,2048]{1,0:T(8,128)(2,1)} %param.22, bf16[16,8,4,128]{3,2,1,0:T(4,128)(2,1)S(1)} %bitcast.128), kind=kOutput, calls=%fused_computation.38 | convolution fusion | flops 268435456 | bytes 3276800 | tf_op jit(solution)/shard_map/dot_general | solution.py:553
  47.4 1.4 select_convert_fusion.mix_ref
  48.8 0.4 collective-permute-start.3
  49.2 1.0 fusion.12.place_ref
  50.3 1.1 constant_dynamic-slice_fusion
  51.3 1.2 copy.50
  52.6 1.2 fusion.9
  54.5 0.4 multiply_reduce_fusion
  54.9 1.1 multiply_convert_fusion.x_ref
  56.0 90.1 %ring_experts_3.1 = bf16[128,2048]{1,0:T(8,128)(2,1)} custom-call(bf16[128,2048]{1,0:T(8,128)(2,1)} %multiply_convert_fusion.x_ref, f32[128,2048]{1,0:T(8,128)} %copy-done.1, bf16[8,128,256]{2,1,0:T(8,128)(2,1)} %fusion.12.place_ref, bf16[16,128,128]{2,1,0:T(8,128)(2,1)} %select_convert_fusion.mix_ref, bf16[704,2048]{1,0:T(8,128)(2,1)} %bitcast.143, ...), custom_call_target="tpu_custom_call" | custom-call | flops 8858370048 | bytes 134217728 | tf_op jit(solution)/shard_map/ring_experts_3/pallas_call | solution.py:433
  146.1 2.4 %copy.104 = bf16[2,64,2048]{2,0,1:T(2,128)(2,1)} copy(bf16[2,64,2048]{2,1,0:T(8,128)(2,1)} %bitcast.130) | data formatting | bytes 1048576 | tf_op jit(solution)/shard_map/reshape | solution.py:602
  (57 shorter events, 2.2 us)
Async XLA Ops:
  0.0 5.4 %copy-start = (bf16[4,512,128]{2,1,0:T(8,128)(2,1)S(1)}, bf16[4,512,128]{2,1,0:T(8,128)(2,1)}, u32[]{:S(2)}) copy-start(bf16[4,512,128]{2,1,0:T(8,128)(2,1)} %param.21) | copy-start | bytes 1572868
  2.4 6.5 %copy-start.9 = (bf16[1,64,2,6]{1,2,3,0:T(2,128)(2,1)S(1)}, bf16[1,64,2,6]{1,2,3,0:T(2,128)(2,1)}, u32[]{:S(2)}) copy-start(bf16[1,64,2,6]{1,2,3,0:T(2,128)(2,1)} %param.19) | copy-start | bytes 4612
  2.4 6.6 %copy-start.7 = (s32[1,64,2,6]{1,2,3,0:T(2,128)S(1)}, s32[1,64,2,6]{1,2,3,0:T(2,128)}, u32[]{:S(2)}) copy-start(s32[1,64,2,6]{1,2,3,0:T(2,128)} %param.18) | copy-start | bytes 9220
  2.4 6.7 %copy-start.5 = (bf16[1,64,2,512]{3,2,1,0:T(2,128)(2,1)S(1)}, bf16[1,64,2,512]{3,2,1,0:T(2,128)(2,1)}, u32[]{:S(2)}) copy-start(bf16[1,64,2,512]{3,2,1,0:T(2,128)(2,1)} %param.15) | copy-start | bytes 393220
  2.4 46.4 %collective-permute-start.1 = (bf16[256,2048]{1,0:T(8,128)(2,1)}, bf16[256,2048]{1,0:T(8,128)(2,1)S(1)}, u32[]{:S(2)}, u32[]{:S(2)}) collective-permute-start(bf16[256,2048]{1,0:T(8,128)(2,1)} %constant_dynamic-slice_fusion.1), channel_id=1, source_target_pairs={{0,16},{16,0},{1,17},{17,1},{2,18},{18,2},{3,19},{19,3},{4,20},{20... | collective-permute-start | bytes 3145736 | tf_op jit(solution)/shard_map/ppermute | solution.py:508
  5.4 44.7 %collective-permute-start = (bf16[2,512,128]{2,1,0:T(8,128)(2,1)S(1)}, bf16[2,512,128]{2,1,0:T(8,128)(2,1)}, u32[]{:S(2)}, u32[]{:S(2)}) collective-permute-start(bf16[2,512,128]{2,1,0:T(8,128)(2,1)S(1)} %constant_dynamic-slice_fusion.3), channel_id=1, source_target_pairs={{0,16},{16,0},{1,17},{17,1},{2,18},{18,2},{3,19},{19,3},{4,20},{20... | collective-permute-start | bytes 786440 | tf_op jit(solution)/shard_map/ppermute | solution.py:507
  33.5 1.6 %slice-start = ((bf16[16,144,512]{2,1,0:T(8,128)(2,1)}), bf16[16,128,512]{2,1,0:T(8,128)(2,1)S(1)}, s32[]{:S(2)}) async-start(bf16[16,144,512]{2,1,0:T(8,128)(2,1)} %ring_gather_0.1), calls=%async_computation | async-start | bytes 4194304 | tf_op jit(solution)/shard_map/slice | solution.py:530
  33.5 3.1 %copy-start.6 = (bf16[1,32,2,512]{3,2,1,0:T(2,128)(2,1)S(1)}, bf16[1,32,2,512]{3,2,1,0:T(2,128)(2,1)}, u32[]{:S(2)}) copy-start(bf16[1,32,2,512]{3,2,1,0:T(2,128)(2,1)} %param.16) | copy-start | bytes 196612
  33.5 3.1 %copy-start.3 = (bf16[2,8,64,512]{3,2,1,0:T(8,128)(2,1)S(1)}, bf16[2,8,64,512]{3,2,1,0:T(8,128)(2,1)}, u32[]{:S(2)}) copy-start(bf16[2,8,64,512]{3,2,1,0:T(8,128)(2,1)} %copy.54) | copy-start | bytes 3145732
  33.5 3.1 %copy-start.10 = (s32[1,2]{1,0:T(1,128)S(1)}, s32[1,2]{1,0:T(1,128)}, u32[]{:S(2)}) copy-start(s32[1,2]{1,0:T(1,128)} %param.17) | copy-start | bytes 28
  40.4 1.6 %copy-start.2 = (bf16[2,16,64,512]{3,2,1,0:T(8,128)(2,1)S(1)}, bf16[2,16,64,512]{3,2,1,0:T(8,128)(2,1)}, u32[]{:S(2)}) copy-start(bf16[2,16,64,512]{3,2,1,0:T(8,128)(2,1)} %copy.53) | copy-start | bytes 6291460
  42.0 2.8 %slice-start.1 = ((bf16[16,144,512]{2,1,0:T(8,128)(2,1)}), bf16[16,16,512]{2,1,0:T(8,128)(2,1)S(1)}, s32[]{:S(2)}) async-start(bf16[16,144,512]{2,1,0:T(8,128)(2,1)} %ring_gather_0.1), calls=%async_computation.1 | async-start | bytes 524288 | tf_op jit(solution)/shard_map/slice | solution.py:577
  43.7 1.0 copy-start.4
  45.3 7.2 %copy-start.8 = (bf16[2048]{0:T(1024)(128)(2,1)S(1)}, bf16[2048]{0:T(1024)(128)(2,1)}, u32[]{:S(2)}) copy-start(bf16[2048]{0:T(1024)(128)(2,1)} %param.20) | copy-start | bytes 12292
  48.8 5.7 %collective-permute-start.3 = (bf16[256,2048]{1,0:T(8,128)(2,1)S(1)}, bf16[256,2048]{1,0:T(8,128)(2,1)S(1)}, u32[]{:S(2)}, u32[]{:S(2)}) collective-permute-start(bf16[256,2048]{1,0:T(8,128)(2,1)S(1)} %collective-permute-done.1), channel_id=1, source_target_pairs={{0,1},{1,0},{2,3},{3,2},{4,5},{5,4},{6,7},{7,6},{8,9},{9,8},{10,11... | collective-permute-start | bytes 3145736 | tf_op jit(solution)/shard_map/ppermute | solution.py:510
  50.1 3.7 %collective-permute-start.2 = (bf16[2,512,128]{2,1,0:T(8,128)(2,1)}, bf16[2,512,128]{2,1,0:T(8,128)(2,1)S(1)}, u32[]{:S(2)}, u32[]{:S(2)}) collective-permute-start(bf16[2,512,128]{2,1,0:T(8,128)(2,1)} %collective-permute-done), channel_id=1, source_target_pairs={{0,1},{1,0},{2,3},{3,2},{4,5},{5,4},{6,7},{7,6},{8,9},{9,8},{10,11... | collective-permute-start | bytes 786440 | tf_op jit(solution)/shard_map/ppermute | solution.py:509
  54.9 1.2 copy-start.1

commit v2 on v1

--- a/solution.py
+++ b/solution.py
@@ -262,72 +262,315 @@
     )(rows_in, mix)
 
 
-def expert_kernel(
-    n, x_ref, keep_ref, place_ref, mix_ref, gate_hbm, up_hbm, down_hbm, out_ref,
-    rows, w_gate, w_up, w_down, act, mine, paired, give, arrived,
-    load_sem, gather_send, gather_recv, swap_send, swap_recv, ring_send, ring_recv, pair_send, pair_recv,
+def layer_kernel(
+    n, table_ref, limit_ref, gain_ref,
+    latent_hbm, query_hbm, memory_hbm, hidden_hbm, uv_hbm, wout_hbm, gate_hbm, up_hbm, down_hbm,
+    out_hbm,
+    latent, query, memory, hidden, keys, tables, heads, scores, probs, top, attended, values, w_uv, w_out, kept,
+    place, mix, rows, w_gate, w_up, w_down, act, mine, paired, give, arrived, produced,
+    load_sem, far_send, far_recv, near_send, near_recv,
+    key_send, key_recv, key_swap_send, key_swap_recv,
+    row_send, row_recv, row_swap_send, row_swap_recv,
+    ring_send, ring_recv, pair_send, pair_recv,
 ):
-    f32 = jnp.float32
+    f32, bf16 = jnp.float32, jnp.bfloat16
     chips = n // 2
     half_ring = chips // 2
-    count, width = x_ref.shape
-    half = count // 2
-    slots = place_ref.shape[1]
     last = chips - 2
+    count, width = kept.shape
+    seqs, span_len = 2, count // 2
+    lat_width = latent.shape[1]
+    mem_len = memory.shape[0] // 2
+    head_count = query.shape[1] // lat_width
+    mem_at = n * span_len
+    key_total = keys.shape[1]
+    here = uv_hbm.shape[0]
+    value_dim = uv_hbm.shape[2]
+    half_here = here // 2
+    slots = place.shape[1]
     me, core, device = ring_place(n)
+    own_dp = lax.axis_index("dp")
+    far_dp = 1 - own_dp
     partner = device(0, 1 - core)
     ahead = (device(1, core), device(-1, core))
-    spans = (pl.ds(0, half), pl.ds(half, half))
+    spans = (pl.ds(0, span_len), pl.ds(span_len, span_len))
+
     loads = [
         pltpu.make_async_copy(src, dst, load_sem.at[i])
-        for i, (src, dst) in enumerate(((gate_hbm, w_gate), (up_hbm, w_up), (down_hbm, w_down)))
+        for i, (src, dst) in enumerate((
+            (latent_hbm.reshape(count, lat_width), latent),
+            (query_hbm.reshape(query.shape), query),
+            (memory_hbm.reshape(memory.shape), memory),
+            (uv_hbm, w_uv.at[pl.ds(own_dp * here, here)]),
+            (hidden_hbm.reshape(count, width), hidden),
+            (wout_hbm, w_out.at[pl.ds(own_dp * here * value_dim, here * value_dim)]),
+            (gate_hbm, w_gate),
+            (up_hbm, w_up),
+            (down_hbm, w_down),
+        ))
     ]
     for load in loads:
         load.start()
-    greet((ahead[0], ahead[1], partner))
     waits = []
 
     def send(copy):
         copy.start()
         waits.append(copy)
 
+    barrier = pltpu.get_barrier_semaphore()
+    for target in (ahead[0], ahead[1], partner):
+        pl.semaphore_signal(barrier, inc=1, device_id={"expert": target}, device_id_type=MESH)
+    pl.semaphore_signal(barrier, inc=1, device_id={"dp": far_dp}, device_id_type=MESH)
+    pl.semaphore_wait(barrier, 4)
+
+    def uv_piece(owner, of_core):
+        return pl.ds(owner * here + of_core * half_here, half_here)
+
+    pieces = far_send.shape[0] - 1
+    out_rows = half_here * value_dim // pieces
+
+    def out_piece(owner, of_core, i):
+        first = (owner * here + of_core * half_here) * value_dim + i * out_rows
+        return pl.ds(pl.multiple_of(first, out_rows), out_rows)
+
+    def across(src, dst, i):
+        return pltpu.make_async_remote_copy(
+            src_ref=src, dst_ref=dst, send_sem=far_send.at[i], recv_sem=far_recv.at[i],
+            device_id={"dp": far_dp}, device_id_type=MESH,
+        )
+
+    send(across(uv_hbm.at[pl.ds(core * half_here, half_here)], w_uv.at[uv_piece(own_dp, core)], 0))
+    for i in range(pieces):
+        source = wout_hbm.at[pl.ds(pl.multiple_of(core * half_here * value_dim + i * out_rows, out_rows), out_rows)]
+        send(across(source, w_out.at[out_piece(own_dp, core, i)], i + 1))
+
+    def far_ref(i, of_core):
+        return w_uv.at[uv_piece(far_dp, of_core)] if i == 0 else w_out.at[out_piece(far_dp, of_core, i - 1)]
+
+    def pass_far(i):
+        piece = far_ref(i, core)
+        across(piece, piece, i).wait_recv()
+        send(remote(piece, piece, near_send.at[i], near_recv.at[i], partner))
+
+    def await_near(i):
+        piece = far_ref(i, 1 - core)
+        remote(piece, piece, near_send.at[i], near_recv.at[i], partner).wait_recv()
+
     def step_of(way, j):
         return (half_ring, way) if j == last else (j // 2 + 1, j % 2)
 
     def offset(way, dist):
         return dist if way == 0 else chips - dist
 
-    for j in (0, 1):
-        for way in (0, 1):
-            send(remote(
-                x_ref.at[spans[j]], rows.at[me, spans[j]],
-                gather_send.at[way, j], gather_recv.at[way, j], ahead[way],
-            ))
-    send(remote(x_ref, rows.at[me], swap_send.at[2 * last + 2], swap_recv.at[2 * last + 2], partner))
-    rows[me] = x_ref[...]
+    def gather(parts, sends, recvs, swap_sends, swap_recvs):
+        own = 2 * last + 2
+
+        def start():
+            for j in (0, 1):
+                for way in (0, 1):
+                    for i, ref in enumerate(parts(me, j)):
+                        send(remote(ref, ref, sends.at[i, way, j], recvs.at[i, way, j], ahead[way]))
+            for h in (0, 1):
+                for i, ref in enumerate(parts(me, h)):
+                    send(remote(ref, ref, swap_sends.at[i, own + h], swap_recvs.at[i, own + h], partner))
+
+        def near_own():
+            for h in (0, 1):
+                for i, ref in enumerate(parts(partner, h)):
+                    remote(ref, ref, swap_sends.at[i, own + h], swap_recvs.at[i, own + h], partner).wait_recv()
+
+        def hop(j):
+            onward = [j + 2, j + 2]
+            if last - 2 <= j < last:
+                onward = [last if j == last - 2 + way else None for way in (0, 1)]
+            if j == last:
+                onward = [None, None]
+            for way in (0, 1):
+                dist, h = step_of(way, j)
+                for i, ref in enumerate(parts(device(-dist if way == 0 else dist, core), h)):
+                    remote(ref, ref, sends.at[i, way, j], recvs.at[i, way, j], ahead[way]).wait_recv()
+                    if onward[way] is not None:
+                        k = onward[way]
+                        send(remote(ref, ref, sends.at[i, way, k], recvs.at[i, way, k], ahead[way]))
+                    k = 2 * j + way
+                    send(remote(ref, ref, swap_sends.at[i, k], swap_recvs.at[i, k], partner))
+
+        def near(j):
+            for way in (0, 1):
+                dist, h = step_of(way, j)
+                k = 2 * j + way
+                for i, ref in enumerate(parts(device(-dist if way == 0 else dist, 1 - core), h)):
+                    remote(ref, ref, swap_sends.at[i, k], swap_recvs.at[i, k], partner).wait_recv()
+
+        return start, near_own, hop, near
+
+    def split_of(total):
+        to = lax.broadcasted_iota(jnp.int32, (total, total), 0)
+        at = lax.broadcasted_iota(jnp.int32, (total, total), 1)
+        return (to == at % 2 * (total // 2) + at // 2).astype(f32).astype(bf16)
+
+    split = split_of(count)
+    to = lax.broadcasted_iota(jnp.int32, (count, count), 0)
+    at = lax.broadcasted_iota(jnp.int32, (count, count), 1)
+    weave = (at == to % 2 * span_len + to // 2).astype(f32).astype(bf16)
+
+    def place_of(slot):
+        return pl.ds(pl.multiple_of(slot * span_len, span_len), span_len)
+
+    def key_parts(slot, h):
+        return [keys.at[h, place_of(slot)]] + ([tables.at[slot]] if h == 0 else [])
+
+    key_start, key_near_own, key_hop, key_near = gather(key_parts, key_send, key_recv, key_swap_send, key_swap_recv)
+    tables[me] = jnp.dot(table_ref[...], split, preferred_element_type=f32).astype(bf16)
+    loads[0].wait()
+    parted = jnp.dot(split, latent[...], preferred_element_type=f32).astype(bf16)
+    for s in range(seqs):
+        keys[s, place_of(me)] = parted[s * span_len : (s + 1) * span_len]
+    key_start()
+
+    loads[1].wait()
+    for s in range(seqs):
+        parted = jnp.dot(
+            split[s * span_len : (s + 1) * span_len], query[...], preferred_element_type=f32
+        ).astype(bf16)
+        for h in range(head_count):
+            heads[s, pl.ds(h * span_len, span_len)] = parted[:, h * lat_width : (h + 1) * lat_width]
+    loads[2].wait()
+    parted = jnp.dot(split_of(2 * mem_len), memory[...], preferred_element_type=f32).astype(bf16)
+    lanes = 2 * span_len
+    row_count = head_count * span_len
+    own_pos = me * span_len + lax.broadcasted_iota(jnp.int32, (row_count, lanes), 0) % span_len
+    lane = lax.broadcasted_iota(jnp.int32, (row_count, lanes), 1)
+    along = (((1,), (1,)), ((), ()))
+    for s in range(seqs):
+        keys[s, pl.ds(mem_at, mem_len)] = parted[s * mem_len : (s + 1) * mem_len]
+        keys[s, pl.ds(mem_at + mem_len, key_total - mem_at - mem_len)] = jnp.zeros(
+            (key_total - mem_at - mem_len, lat_width), bf16
+        )
+        score = lax.dot_general(heads[s], keys[s, pl.ds(mem_at, lanes)], along, preferred_element_type=f32)
+        score = jnp.where(lane < mem_len, score, -jnp.inf)
+        scores[s, :, pl.ds(mem_at, lanes)] = score
+        top[s] = score
+
+    def score_chip(k):
+        first = pl.multiple_of(device(k, 0) * span_len, lanes)
+        for s in range(seqs):
+            score = lax.dot_general(heads[s], keys[s, pl.ds(first, lanes)], along, preferred_element_type=f32)
+            pos = first + lane
+            visible = (pos <= own_pos) & (pos < limit_ref[pl.ds(s, 1)])
+            score = jnp.where(visible, score, -jnp.inf)
+            scores[s, :, pl.ds(first, lanes)] = score
+            top[s] = jnp.maximum(top[s], score)
+
+    tasks = [key_near_own, functools.partial(score_chip, 0)]
+    for j in range(last + 1):
+        key_hop(j)
+        for task in tasks:
+            task()
+        tasks = [functools.partial(key_near, j)]
+        if j == 3:
+            loads[3].wait()
+            pass_far(0)
+        if j % 2 == 1 or j == last:
+            dist = step_of(0, j)[0]
+            ks = [half_ring] if j == last else [dist, chips - dist]
+            tasks += [functools.partial(score_chip, k) for k in ks]
+    for task in tasks:
+        task()
+    pass_far(1)
+
+    scale = score_scale * 1.4426950408889634
+    block = 64
+
+    for s in range(seqs):
+        top[s, :, pl.ds(0, 1)] = jnp.max(top[s], axis=1, keepdims=True)
+
+        def soften(i, carry, s=s):
+            part = pl.ds(pl.multiple_of(i * block, block), block)
+            shifted = (scores[s, part] - top[s, part, pl.ds(0, 1)]) * scale
+            weight = jnp.exp2(shifted)
+            probs[part] = weight.astype(bf16)
+            top[s, part, pl.ds(0, 1)] = 1.0 / jnp.sum(weight, axis=1, keepdims=True)
+            return carry
+
+        lax.fori_loop(0, row_count // block, soften, 0)
+        blend = jnp.dot(probs[...], keys[s], preferred_element_type=f32)
+        attended[s] = (blend * top[s, :, pl.ds(0, 1)]).astype(bf16)
+        if s == 0:
+            pass_far(2)
+    await_near(0)
+    for h in range(head_count):
+        part = pl.ds(h * span_len, span_len)
+        both = jnp.concatenate([attended[0, part], attended[1, part]], axis=0)
+        values[:, pl.ds(h * value_dim, value_dim)] = jnp.dot(
+            both, w_uv[h], preferred_element_type=f32
+        ).astype(bf16)
+    woven = jnp.dot(weave, values[...], preferred_element_type=f32).astype(bf16)
+    values[...] = woven
+    loads[4].wait()
+    loads[5].wait()
+    depth = here * value_dim
+    near_cols = pl.ds(pl.multiple_of(own_dp * depth, depth), depth)
+    far_cols = pl.ds(pl.multiple_of(far_dp * depth, depth), depth)
+    kept[...] = hidden[...].astype(f32) + jnp.dot(values[:, near_cols], w_out[near_cols], preferred_element_type=f32)
+    for i in range(3, pieces + 1):
+        pass_far(i)
+    for i in range(1, pieces + 1):
+        await_near(i)
+    residual = kept[...] + jnp.dot(values[:, far_cols], w_out[far_cols], preferred_element_type=f32)
+    kept[...] = residual
+    mean_square = jnp.mean(residual * residual, axis=1, keepdims=True)
+    rows[me] = (residual * lax.rsqrt(mean_square + norm_eps) * gain_ref[...].astype(f32)).astype(bf16)
+
+    def row_parts(slot, h):
+        return [rows.at[slot, spans[h]]]
+
+    row_start, row_near_own, row_hop, row_near = gather(row_parts, row_send, row_recv, row_swap_send, row_swap_recv)
+    row_start()
+
+    hits, gates = [], []
+    own_id = me.astype(f32)
+    for c in range(chips):
+        pair = jnp.concatenate([tables[2 * c], tables[2 * c + 1]], axis=1).astype(f32)
+        matches = pair[:8] == own_id
+        hits.append(jnp.max(jnp.where(matches, 1.0, 0.0), axis=0, keepdims=True))
+        gates.append(jnp.sum(jnp.where(matches, pair[8:], 0.0), axis=0, keepdims=True))
+    hits = jnp.concatenate(hits, axis=0)
+    to = lax.broadcasted_iota(jnp.int32, (2 * count, 2 * count), 0)
+    at = lax.broadcasted_iota(jnp.int32, (2 * count, 2 * count), 1)
+    earlier = (to < at).astype(f32).astype(bf16)
+    ranks = jnp.dot(hits.astype(bf16), earlier, preferred_element_type=f32)
+    ranks = jnp.where(hits > 0.5, ranks, -1.0)
+    slot_id = lax.broadcasted_iota(jnp.int32, (slots, 2 * count), 0).astype(f32)
+    for c in range(chips):
+        chosen = slot_id == ranks[c : c + 1]
+        place[c] = jnp.where(chosen, 1.0, 0.0).astype(bf16)
+        weighed = jnp.where(chosen, gates[c], 0.0).astype(bf16)
+        mix[2 * c] = weighed[:, :count]
+        mix[2 * c + 1] = weighed[:, count:]
 
     def start_experts(ks):
         picked = []
         for k in ks:
             first = device(k, 0)
             held = rows[pl.ds(first, 2)].reshape(2 * count, width)
-            picked.append(jnp.dot(place_ref[first // 2], held, preferred_element_type=f32).astype(jnp.bfloat16))
+            picked.append(jnp.dot(place[first // 2], held, preferred_element_type=f32).astype(bf16))
         picked = picked[0] if len(ks) == 1 else jnp.concatenate(picked, axis=0)
-        along = (((1,), (1,)), ((), ()))
         gate_h = lax.dot_general(picked, w_gate[...], along, preferred_element_type=f32)
         up_h = lax.dot_general(picked, w_up[...], along, preferred_element_type=f32)
-        act[pl.ds(0, len(ks) * slots)] = (gate_h / (1.0 + jnp.exp(-gate_h)) * up_h).astype(jnp.bfloat16)
+        act[pl.ds(0, len(ks) * slots)] = (gate_h / (1.0 + jnp.exp(-gate_h)) * up_h).astype(bf16)
 
     shares = {}
+    down = (((0,), (0,)), ((), ()))
 
     def end_experts(ks):
-        made = jnp.dot(act[pl.ds(0, len(ks) * slots)], w_down[...], preferred_element_type=f32).astype(jnp.bfloat16)
+        made = jnp.dot(act[pl.ds(0, len(ks) * slots)], w_down[...], preferred_element_type=f32).astype(bf16)
         for i, k in enumerate(ks):
             part = made[i * slots : (i + 1) * slots]
-            give[k] = jnp.dot(mix_ref[device(k, 1 - core)], part, preferred_element_type=f32).astype(give.dtype)
+            give[k] = lax.dot_general(mix[device(k, 1 - core)], part, down, preferred_element_type=f32).astype(bf16)
             shares[k] = remote(give.at[k], paired.at[k], pair_send.at[k], pair_recv.at[k], partner)
             send(shares[k])
-            mine[k] = jnp.dot(mix_ref[device(k, core)], part, preferred_element_type=f32).astype(mine.dtype)
+            mine[k] = lax.dot_general(mix[device(k, core)], part, down, preferred_element_type=f32).astype(bf16)
 
     seen = set()
 
@@ -353,42 +596,25 @@
                 j = index_of(dist + 1, h)
                 await_ring(way, j)
                 total = total + arrived[way, j].astype(f32)
-            mine[k, spans[h]] = total.astype(mine.dtype)
+            mine[k, spans[h]] = total.astype(bf16)
             j = index_of(dist, h)
             send(remote(
                 mine.at[k, spans[h]], arrived.at[way, j],
                 ring_send.at[way, j], ring_recv.at[way, j], ahead[way],
             ))
 
-    other = rows.at[partner]
-    remote(other, other, swap_send.at[2 * last + 2], swap_recv.at[2 * last + 2], partner).wait_recv()
-    for load in loads:
+    row_near_own()
+    for load in loads[6:]:
         load.wait()
     start_experts([0])
     end_experts([0])
 
     tasks = []
     for j in range(last + 1):
-        for way in (0, 1):
-            dist, h = step_of(way, j)
-            piece = rows.at[device(-dist if way == 0 else dist, core), spans[h]]
-            remote(piece, piece, gather_send.at[way, j], gather_recv.at[way, j], ahead[way]).wait_recv()
-            onward = j + 2
-            if last - 2 <= j < last:
-                onward = last if j == last - 2 + way else None
-            if j == last:
-                onward = None
-            if onward is not None:
-                send(remote(
-                    piece, piece, gather_send.at[way, onward], gather_recv.at[way, onward], ahead[way]
-                ))
-            send(remote(piece, piece, swap_send.at[2 * j + way], swap_recv.at[2 * j + way], partner))
+        row_hop(j)
         if j % 2 == 1 or j == last:
-            for i in ((j - 1, j) if j % 2 == 1 else (j,)):
-                for way in (0, 1):
-                    dist, h = step_of(way, i)
-                    piece = rows.at[device(-dist if way == 0 else dist, 1 - core), spans[h]]
-                    remote(piece, piece, swap_send.at[2 * i + way], swap_recv.at[2 * i + way], partner).wait_recv()
+            for i in (j - 1, j) if j % 2 == 1 else (j,):
+                row_near(i)
             dist = step_of(0, j)[0]
             ks = [half_ring] if j == last else [dist, chips - dist]
             tasks += [functools.partial(start_experts, ks), functools.partial(end_experts, ks)]
@@ -410,59 +636,101 @@
             j = index_of(1, h)
             await_ring(way, j)
             total = total + arrived[way, j].astype(f32)
-        out_ref[spans[h]] = (keep_ref[spans[h]] + total).astype(out_ref.dtype)
+        produced[spans[h]] = (kept[spans[h]] + total).astype(bf16)
+    store = pltpu.make_async_copy(produced, out_hbm.reshape(count, width), load_sem.at[0])
+    store.start()
+    store.wait()
     for copy in waits:
         copy.wait_send()
 
 
-def expert_bytes(n, count, width, inner, slots):
-    chips = n // 2
-    held = n * count * width + 3 * width * inner + 3 * chips * count * width + (chips - 1) * count * width
-    held += 6 * count * width + 2 * chips * slots * 2 * count
-    return 2 * held + 4 * 2 * slots * (2 * inner + 2 * width)
-
-
-def ring_experts(x, keep, place, mix, w_gate_t, w_up_t, w_down, n, collective_id):
-    count, width = x.shape
+def fused_layer(
+    table, limits, gain, latents, queries, memory, hidden, w_uv, w_out, w_gate_t, w_up_t, w_down, n, slots, collective_id
+):
+    span_len, seqs, width = hidden.shape
+    count = span_len * seqs
+    lat_width = latents.shape[2]
+    head_count = queries.shape[2] // lat_width
+    here, _, value_dim = w_uv.shape
+    mem_len = memory.shape[0]
     chips = n // 2
     steps = chips - 1
     inner = w_down.shape[0]
-    slots = place.shape[1]
-    dtype = x.dtype
-    dma = pltpu.SemaphoreType.DMA
+    key_total = n * span_len + count
+    bf16, f32 = jnp.bfloat16, jnp.float32
+    dma, vmem = pltpu.SemaphoreType.DMA, pltpu.VMEM
+    row_count = head_count * span_len
+    pieces = 4
     return pl.pallas_call(
-        functools.partial(expert_kernel, n),
-        out_shape=jax.ShapeDtypeStruct((count, width), dtype),
-        in_specs=[pl.BlockSpec(memory_space=pltpu.VMEM)] * 4 + [pl.BlockSpec(memory_space=pl.ANY)] * 3,
-        out_specs=pl.BlockSpec(memory_space=pltpu.VMEM),
+        functools.partial(layer_kernel, n),
+        out_shape=jax.ShapeDtypeStruct((span_len, seqs, width), bf16),
+        in_specs=[pl.BlockSpec(memory_space=pltpu.VMEM)] * 3 + [pl.BlockSpec(memory_space=pl.ANY)] * 9,
+        out_specs=pl.BlockSpec(memory_space=pl.ANY),
         scratch_shapes=[
-            pltpu.VMEM((n, count, width), dtype),
-            pltpu.VMEM((inner, width), dtype),
-            pltpu.VMEM((inner, width), dtype),
-            pltpu.VMEM((inner, width), dtype),
-            pltpu.VMEM((2 * slots, inner), dtype),
-            pltpu.VMEM((chips, count, width), dtype),
-            pltpu.VMEM((chips, count, width), dtype),
-            pltpu.VMEM((chips, count, width), dtype),
-            pltpu.VMEM((2, steps, count // 2, width), dtype),
-            dma((3,)),
-            dma((2, steps)),
-            dma((2, steps)),
-            dma((2 * steps + 1,)),
-            dma((2 * steps + 1,)),
+            vmem((count, lat_width), bf16),
+            vmem((count, head_count * lat_width), bf16),
+            vmem((seqs * mem_len, lat_width), bf16),
+            vmem((count, width), bf16),
+            vmem((seqs, key_total, lat_width), bf16),
+            vmem((n, 16, count), bf16),
+            vmem((seqs, row_count, lat_width), bf16),
+            vmem((seqs, row_count, key_total), f32),
+            vmem((row_count, key_total), bf16),
+            vmem((seqs, row_count, count), f32),
+            vmem((seqs, row_count, lat_width), bf16),
+            vmem((count, head_count * value_dim), bf16),
+            vmem((head_count, lat_width, value_dim), bf16),
+            vmem((head_count * value_dim, width), bf16),
+            vmem((count, width), f32),
+            vmem((chips, slots, 2 * count), bf16),
+            vmem((n, slots, count), bf16),
+            vmem((n, count, width), bf16),
+            vmem((inner, width), bf16),
+            vmem((inner, width), bf16),
+            vmem((inner, width), bf16),
+            vmem((2 * slots, inner), bf16),
+            vmem((chips, count, width), bf16),
+            vmem((chips, count, width), bf16),
+            vmem((chips, count, width), bf16),
+            vmem((2, steps, count // 2, width), bf16),
+            vmem((count, width), bf16),
+            dma((9,)),
+            dma((pieces + 1,)),
+            dma((pieces + 1,)),
+            dma((pieces + 1,)),
+            dma((pieces + 1,)),
+            dma((2, 2, steps)),
+            dma((2, 2, steps)),
+            dma((2, 2 * steps + 2)),
+            dma((2, 2 * steps + 2)),
+            dma((1, 2, steps)),
+            dma((1, 2, steps)),
+            dma((1, 2 * steps + 2)),
+            dma((1, 2 * steps + 2)),
             dma((2, steps)),
             dma((2, steps)),
             dma((chips,)),
             dma((chips,)),
         ],
         compiler_params=pltpu.CompilerParams(
-            collective_id=collective_id, has_side_effects=True, vmem_limit_bytes=62 * 1024 * 1024
+            collective_id=collective_id, has_side_effects=True, vmem_limit_bytes=67000000
         ),
         cost_estimate=pl.CostEstimate(
             flops=6 * chips * slots * width * inner, bytes_accessed=32 * n * count * width, transcendentals=0
         ),
-        name="ring_experts_%d" % collective_id,
-    )(x, keep, place, mix, w_gate_t, w_up_t, w_down)
+        name="layer_%d" % collective_id,
+    )(table, limits, gain, latents, queries, memory, hidden, w_uv, w_out, w_gate_t, w_up_t, w_down)
+
+
+def layer_bytes(n, count, width, inner, slots, lat_width, head_count, value_dim):
+    chips = n // 2
+    key_total = (n + 2) * count // 2
+    row_count = head_count * count // 2
+    front = count * (1 + head_count) * lat_width + 2 * key_total * lat_width + 4 * row_count * lat_width
+    front += 5 * row_count * key_total + 4 * row_count * count + head_count * value_dim * (lat_width + width + count)
+    back = n * count * width + 3 * width * inner + (4 * chips - 1) * count * width + 5 * count * width
+    back += 4 * chips * slots * count + 2 * slots * inner
+    return 2 * (front + back) + 8 * slots * inner * 2
 
 
 def shards(
@@ -492,6 +760,33 @@
     own_dp = lax.axis_index("dp")
     heads_here, _, value_dim = w_uv.shape
     top_count = ids.shape[3]
+    ids_t = jnp.transpose(ids[0], (2, 1, 0)).reshape(top_count, row_count).astype(bf16)
+    gates_t = jnp.transpose(gates[0], (2, 1, 0)).reshape(top_count, row_count)
+    capacity = min(row_count, row_count * top_count // (n * w_gate.shape[0]) + 2)
+    slots = -(-2 * capacity // 128) * 128
+    fits = (
+        dp_size == 2
+        and w_gate.shape[0] == 1
+        and n >= 8
+        and top_count <= 8
+        and seq_count == 2
+        and row_count % 128 == 0
+        and heads_here % 2 == 0
+        and mem_latents.shape[1] <= row_count
+        and layer_bytes(n, row_count, model_width, w_down.shape[1], slots, latent_dim, head_count, value_dim)
+        < 60 * 1024 * 1024
+    )
+    if fits:
+        pad = ((0, 8 - top_count), (0, 0))
+        table = jnp.concatenate(
+            [jnp.pad(ids_t, pad, constant_values=255), jnp.pad(gates_t, pad)], axis=0
+        )
+        out = fused_layer(
+            table, jnp.broadcast_to(lengths[0][:, None], (seq_count, row_count)), norm_gain[None],
+            latents[0], queries[0], mem_latents[0], hidden[0], w_uv, w_out,
+            jnp.transpose(w_gate[0]), jnp.transpose(w_up[0]), w_down[0], n, slots, 4,
+        )
+        return out[None]
 
     half_heads = heads_here // 2
     uv_half = lax.dynamic_slice_in_dim(w_uv, core * half_heads, half_heads, 0)
@@ -517,8 +812,6 @@
         sizes += [half_heads, half_heads]
 
     latent_rows = jnp.transpose(latents[0], (1, 0, 2)).reshape(row_count, latent_dim)
-    ids_t = jnp.transpose(ids[0], (2, 1, 0)).reshape(top_count, row_count).astype(bf16)
-    gates_t = jnp.transpose(gates[0], (2, 1, 0)).reshape(top_count, row_count)
     table = jnp.concatenate([ids_t, gates_t], axis=0).reshape(-1)
     table_rows = -(-table.shape[0] // (16 * latent_dim)) * 16
     table = jnp.pad(table, (0, table_rows * latent_dim - table.shape[0]))
@@ -559,27 +852,17 @@
     mean_square = jnp.mean(residual * residual, axis=-1, keepdims=True)
     normed = (residual * lax.rsqrt(mean_square + norm_eps) * norm_gain.astype(f32)).astype(bf16)
 
+    rows_all = ring_gather(normed, n, row_count // 2, 1)
     experts_here = w_gate.shape[0]
     expert_count = n * experts_here
-    capacity = min(row_count, row_count * top_count // expert_count + 2)
     groups = n // 2
     wide = 2 * row_count
-    slots = -(-2 * capacity // 128) * 128
-    inner = w_down.shape[1]
-    joined = (
-        experts_here == 1
-        and groups >= 4
-        and row_count % 32 == 0
-        and expert_bytes(n, row_count, model_width, inner, slots) < 52 * 1024 * 1024
-    )
-    if not joined:
-        slots = -(-2 * capacity // 16) * 16
+    slots = -(-2 * capacity // 16) * 16
     tables = gathered[:, row_count:].reshape(n, -1)[:, : 2 * top_count * row_count]
     tables = tables.reshape(groups, 2, 2, top_count, row_count)
     named = jnp.transpose(tables[:, :, 0], (2, 0, 1, 3)).reshape(top_count, groups, wide)
     scale = jnp.transpose(tables[:, :, 1], (2, 0, 1, 3)).reshape(top_count, groups, wide)
-    if not joined:
-        rows_all = ring_gather(normed, n, row_count // 2, 1).reshape(groups, wide, model_width)
+    rows_all = rows_all.reshape(groups, wide, model_width)
     steps = jnp.arange(wide, dtype=jnp.int32)
     earlier = (steps[:, None] < steps[None, :]).astype(bf16)
     made_rows, mixes = [], []
@@ -594,12 +877,6 @@
         slot_t = jnp.where(hit, slot, -1).reshape(n, row_count)
         chosen_t = slot_t[:, :, None] == jnp.arange(slots, dtype=jnp.int32)[None, None, :]
         mixes.append(jnp.where(chosen_t, gate.reshape(n, row_count)[:, :, None], 0.0).astype(bf16))
-        if joined:
-            layer_out = ring_experts(
-                normed, residual, placing, mixes[0],
-                jnp.transpose(w_gate[0]), jnp.transpose(w_up[0]), w_down[0], n, 3,
-            )
-            return jnp.transpose(layer_out.reshape(seq_count, local_len, model_width), (1, 0, 2))[None]
         picked = jnp.einsum("gct,gtd->gcd", placing, rows_all, preferred_element_type=f32)
         picked = picked.astype(bf16).reshape(groups * slots, model_width)
         gate_h = jnp.dot(picked, w_gate[e], preferred_element_type=f32)

time: 149 us -> 135 us (0.906)
  Pallas kernels: 114 us -> 127 us
  local copies, waits for them, and re-layouts: 16 us -> 5.61 us
  matrix products: 10 us -> 0 us
  starting transfers between devices: 3.58 us -> 0 us
  other arithmetic: 4.87 us -> 1.3 us
    pallas_call x2 -> x1, Pallas kernels: 114 us -> 127 us  [fused_layer(): pl.pallas_call(functools.partial(layer_kernel, n), out_shape=jax.ShapeDty...]
    dot_general x9 -> x0, matrix products: 10 us -> none  [the longest x1 3.72 us: shards(): jnp.einsum('sql,sjl->sqj', query_rows, keys, preferred_element_type=f32)]
    transpose x4 -> x0, local copies, waits for them, and re-layouts: 4.32 us -> none  [the longest x1 1.57 us: shards(): jnp.transpose(queries[0].reshape(local_len, seq_count, head_count, latent...]
    ppermute x4 -> x0, starting transfers between devices: 3.58 us -> none  [the longest x1 2.97 us: shards(): out_far = lax.ppermute(out_half, 'dp', turn)]
    dynamic_slice x3 -> x0, local copies, waits for them, and re-layouts: 3.48 us -> none  [the longest x1 2.4 us: shards(): lax.dynamic_slice_in_dim(w_out, core * half_heads * value_dim, half_heads...]
    convert_element_type x4 -> x0, other arithmetic: 3.48 us -> none  [the longest x1 1.4 us: shards(): jnp.where(chosen_t, gate.reshape(n, row_count)[:, :, None], 0.0)]
    broadcast_in_dim x0 -> x2, local copies, waits for them, and re-layouts: none -> 2.56 us  [the longest x1 1.29 us: shards(): norm_gain[None]]
    reshape x3 -> x0, local copies, waits for them, and re-layouts: 2.48 us -> none  [the longest x1 2.37 us: shards(): layer_out.reshape(seq_count, local_len, model_width)]
  transfers between devices with their start and end apart: 4 -> 0, of which waited for: 0 -> 0; matrix products, arithmetic and copies ran while one was open for 14% -> 0% of each run, Pallas kernels for 16% -> 0%
where the time goes in v2:
time: 135 us; the launch traced here: 134 us
  Pallas kernels  127 us (94%)
  local copies, waits for them, and re-layouts  5.61 us (4%)
    pallas_call x1, Pallas kernels, fused_layer(): pl.pallas_call(functools.partial(layer_kernel, n), out_shape=jax.ShapeDty...  127 us

profile of v2, /device:TPU:0, one launch (start us, length us, event | category | flops | bytes accessed | tf_op | source)
XLA Modules:
  0.0 134.3 jit_solution(16634048133046480428)
XLA Ops:
  0.0 1.3 broadcast_in_dim.14.limit_ref
  1.3 0.8 reshape.7
  2.0 0.7 convert_bitcast_fusion
  2.7 0.1 convert_element_type.18
  2.8 0.6 fusion.2.table_ref
  3.4 1.3 broadcast_in_dim.15.gain_ref
  4.7 127.4 %layer_4.1 = bf16[64,2,2048]{2,1,0:T(2,128)(2,1)} custom-call(bf16[16,128]{1,0:T(8,128)(2,1)} %fusion.2.table_ref, s32[2,128]{1,0:T(2,128)} %broadcast_in_dim.14.limit_ref, bf16[1,2048]{1,0:T(2,128)(2,1)} %broadcast_in_dim.15.gain_ref, bf16[64,2,512]{2,1,0:T(2,128)(2,1)} %bitcast.27, bf16[64,2,4096]{2,1,0:T(2,128)(2,1)} %bitcast.25, ...), custom_call_target="tpu_custom_call" | custom-call | flops 8858370048 | bytes 134217728 | tf_op jit(solution)/shard_map/layer_4/pallas_call | solution.py:664
  132.1 2.2 %copy.15 = bf16[1,64,2,2048]{3,2,1,0:T(2,128)(2,1)} copy(bf16[1,64,2,2048]{3,2,1,0:T(2,128)(2,1)} %bitcast.20) | data formatting | bytes 1048576

commit v3 on v2

--- a/solution.py
+++ b/solution.py
@@ -263,14 +263,18 @@
 
 
 def layer_kernel(
-    n, table_ref, limit_ref, gain_ref,
+    n,
+    ids_hbm, gates_hbm, limit_hbm, gain_hbm,
     latent_hbm, query_hbm, memory_hbm, hidden_hbm, uv_hbm, wout_hbm, gate_hbm, up_hbm, down_hbm,
     out_hbm,
-    latent, query, memory, hidden, keys, tables, heads, scores, probs, top, attended, values, w_uv, w_out, kept,
+    ids, gates, limit, gain,
+    latent, query, memory, hidden, parted_hidden, keys, tables, heads, bound, peak, mass, blend,
+    attended, values, w_uv, w_out, kept,
     place, mix, rows, w_gate, w_up, w_down, act, mine, paired, give, arrived, produced,
     load_sem, far_send, far_recv, near_send, near_recv,
     key_send, key_recv, key_swap_send, key_swap_recv,
     row_send, row_recv, row_swap_send, row_swap_recv,
+    round_send, round_recv, round_swap_send, round_swap_recv,
     ring_send, ring_recv, pair_send, pair_recv,
 ):
     f32, bf16 = jnp.float32, jnp.bfloat16
@@ -284,6 +288,7 @@
     head_count = query.shape[1] // lat_width
     mem_at = n * span_len
     key_total = keys.shape[1]
+    top_count = ids.shape[0]
     here = uv_hbm.shape[0]
     value_dim = uv_hbm.shape[2]
     half_here = here // 2
@@ -299,6 +304,10 @@
         pltpu.make_async_copy(src, dst, load_sem.at[i])
         for i, (src, dst) in enumerate((
             (latent_hbm.reshape(count, lat_width), latent),
+            (ids_hbm, ids),
+            (gates_hbm, gates),
+            (limit_hbm, limit),
+            (gain_hbm, gain),
             (query_hbm.reshape(query.shape), query),
             (memory_hbm.reshape(memory.shape), memory),
             (uv_hbm, w_uv.at[pl.ds(own_dp * here, here)]),
@@ -326,12 +335,18 @@
     def uv_piece(owner, of_core):
         return pl.ds(owner * here + of_core * half_here, half_here)
 
-    pieces = far_send.shape[0] - 1
-    out_rows = half_here * value_dim // pieces
-
-    def out_piece(owner, of_core, i):
-        first = (owner * here + of_core * half_here) * value_dim + i * out_rows
-        return pl.ds(pl.multiple_of(first, out_rows), out_rows)
+    depth = here * value_dim
+    round_rows = round_share(depth, n)
+    pieces = far_send.shape[0] - 3
+    out_rows = (depth - n * round_rows) // (2 * pieces)
+
+    def out_piece(first, of_core, i):
+        at = first + n * round_rows + (of_core * pieces + i) * out_rows
+        return pl.ds(pl.multiple_of(at, 8), out_rows)
+
+    def round_piece(first, slot, h):
+        size = round_rows // 2
+        return pl.ds(pl.multiple_of(first + slot * round_rows + h * size, 8), size)
 
     def across(src, dst, i):
         return pltpu.make_async_remote_copy(
@@ -339,13 +354,14 @@
             device_id={"dp": far_dp}, device_id_type=MESH,
         )
 
+    for h in (0, 1):
+        send(across(wout_hbm.at[round_piece(0, me, h)], w_out.at[round_piece(own_dp * depth, me, h)], pieces + 1 + h))
     send(across(uv_hbm.at[pl.ds(core * half_here, half_here)], w_uv.at[uv_piece(own_dp, core)], 0))
     for i in range(pieces):
-        source = wout_hbm.at[pl.ds(pl.multiple_of(core * half_here * value_dim + i * out_rows, out_rows), out_rows)]
-        send(across(source, w_out.at[out_piece(own_dp, core, i)], i + 1))
+        send(across(wout_hbm.at[out_piece(0, core, i)], w_out.at[out_piece(own_dp * depth, core, i)], i + 1))
 
     def far_ref(i, of_core):
-        return w_uv.at[uv_piece(far_dp, of_core)] if i == 0 else w_out.at[out_piece(far_dp, of_core, i - 1)]
+        return w_uv.at[uv_piece(far_dp, of_core)] if i == 0 else w_out.at[out_piece(far_dp * depth, of_core, i - 1)]
 
     def pass_far(i):
         piece = far_ref(i, core)
@@ -365,14 +381,12 @@
     def gather(parts, sends, recvs, swap_sends, swap_recvs):
         own = 2 * last + 2
 
-        def start():
-            for j in (0, 1):
-                for way in (0, 1):
-                    for i, ref in enumerate(parts(me, j)):
-                        send(remote(ref, ref, sends.at[i, way, j], recvs.at[i, way, j], ahead[way]))
-            for h in (0, 1):
+        def start(h):
+            for way in (0, 1):
                 for i, ref in enumerate(parts(me, h)):
-                    send(remote(ref, ref, swap_sends.at[i, own + h], swap_recvs.at[i, own + h], partner))
+                    send(remote(ref, ref, sends.at[i, way, h], recvs.at[i, way, h], ahead[way]))
+            for i, ref in enumerate(parts(me, h)):
+                send(remote(ref, ref, swap_sends.at[i, own + h], swap_recvs.at[i, own + h], partner))
 
         def near_own():
             for h in (0, 1):
@@ -414,127 +428,166 @@
     at = lax.broadcasted_iota(jnp.int32, (count, count), 1)
     weave = (at == to % 2 * span_len + to // 2).astype(f32).astype(bf16)
 
-    def place_of(slot):
-        return pl.ds(pl.multiple_of(slot * span_len, span_len), span_len)
+    def place_of(slot, first, size):
+        return pl.ds(pl.multiple_of(slot * span_len + first, size), size)
+
+    sub = span_len // 2
 
     def key_parts(slot, h):
-        return [keys.at[h, place_of(slot)]] + ([tables.at[slot]] if h == 0 else [])
+        found = [keys.at[h, place_of(slot, i * sub, sub)] for i in (0, 1)]
+        return found + ([tables.at[slot]] if h == 0 else [])
 
     key_start, key_near_own, key_hop, key_near = gather(key_parts, key_send, key_recv, key_swap_send, key_swap_recv)
-    tables[me] = jnp.dot(table_ref[...], split, preferred_element_type=f32).astype(bf16)
-    loads[0].wait()
-    parted = jnp.dot(split, latent[...], preferred_element_type=f32).astype(bf16)
+    for load in loads[:5]:
+        load.wait()
+    lines = []
+    for source, filler in ((ids, 255.0), (gates, 0.0)):
+        taken = source[...].astype(f32)
+        lines.append(jnp.concatenate([taken[:, s, :] for s in range(seqs)], axis=1))
+        if top_count < 8:
+            lines.append(jnp.full((8 - top_count, count), filler, f32))
+    tables[me] = jnp.concatenate(lines, axis=0).astype(bf16)
     for s in range(seqs):
-        keys[s, place_of(me)] = parted[s * span_len : (s + 1) * span_len]
-    key_start()
-
-    loads[1].wait()
+        keys[s, place_of(me, 0, span_len)] = jnp.dot(
+            split[s * span_len : (s + 1) * span_len], latent[...], preferred_element_type=f32
+        ).astype(bf16)
+        key_start(s)
+
+    loads[5].wait()
     for s in range(seqs):
         parted = jnp.dot(
             split[s * span_len : (s + 1) * span_len], query[...], preferred_element_type=f32
         ).astype(bf16)
         for h in range(head_count):
             heads[s, pl.ds(h * span_len, span_len)] = parted[:, h * lat_width : (h + 1) * lat_width]
-    loads[2].wait()
+    loads[6].wait()
     parted = jnp.dot(split_of(2 * mem_len), memory[...], preferred_element_type=f32).astype(bf16)
     lanes = 2 * span_len
     row_count = head_count * span_len
+    lane = lax.broadcasted_iota(jnp.int32, (row_count, lanes), 1)
     own_pos = me * span_len + lax.broadcasted_iota(jnp.int32, (row_count, lanes), 0) % span_len
-    lane = lax.broadcasted_iota(jnp.int32, (row_count, lanes), 1)
     along = (((1,), (1,)), ((), ()))
+    scale = score_scale * 1.4426950408889634
     for s in range(seqs):
         keys[s, pl.ds(mem_at, mem_len)] = parted[s * mem_len : (s + 1) * mem_len]
         keys[s, pl.ds(mem_at + mem_len, key_total - mem_at - mem_len)] = jnp.zeros(
             (key_total - mem_at - mem_len, lat_width), bf16
         )
-        score = lax.dot_general(heads[s], keys[s, pl.ds(mem_at, lanes)], along, preferred_element_type=f32)
-        score = jnp.where(lane < mem_len, score, -jnp.inf)
-        scores[s, :, pl.ds(mem_at, lanes)] = score
-        top[s] = score
-
-    def score_chip(k):
-        first = pl.multiple_of(device(k, 0) * span_len, lanes)
+        bound[s] = jnp.minimum(own_pos, limit[:, s : s + 1] - 1) - lane
+
+    def wide(x, times):
+        return x if times == 1 else jnp.concatenate([x] * times, axis=1)
+
+    def attend(ks, opening=False):
+        firsts = [pl.multiple_of(device(k, 0) * span_len, lanes) for k in ks]
         for s in range(seqs):
-            score = lax.dot_general(heads[s], keys[s, pl.ds(first, lanes)], along, preferred_element_type=f32)
-            pos = first + lane
-            visible = (pos <= own_pos) & (pos < limit_ref[pl.ds(s, 1)])
-            score = jnp.where(visible, score, -jnp.inf)
-            scores[s, :, pl.ds(first, lanes)] = score
-            top[s] = jnp.maximum(top[s], score)
-
-    tasks = [key_near_own, functools.partial(score_chip, 0)]
+            held = [keys[s, pl.ds(first, lanes)] for first in firsts]
+            seen_keys = [first <= bound[s] for first in firsts]
+            if opening:
+                held.append(keys[s, pl.ds(mem_at, lanes)])
+                seen_keys.append(lane < mem_len)
+            held = held[0] if len(held) == 1 else jnp.concatenate(held, axis=0)
+            score = lax.dot_general(heads[s], held, along, preferred_element_type=f32)
+            parts = [
+                jnp.where(visible, score[:, i * lanes : (i + 1) * lanes], -jnp.inf)
+                for i, visible in enumerate(seen_keys)
+            ]
+            top = functools.reduce(jnp.maximum, parts)
+            top = jnp.broadcast_to(jnp.max(top, axis=1, keepdims=True), top.shape)
+            if not opening:
+                before = peak[s]
+                top = jnp.maximum(before, top)
+                fade = jnp.exp2((before - top) * scale)
+            parts = [jnp.exp2((part - top) * scale) for part in parts]
+            added = functools.reduce(jnp.add, parts)
+            mass[s] = added if opening else mass[s] * fade + added
+            peak[s] = top
+            weight = parts[0] if len(parts) == 1 else jnp.concatenate(parts, axis=1)
+            more = jnp.dot(weight.astype(bf16), held, preferred_element_type=f32)
+            blend[s] = more if opening else blend[s] * wide(fade, lat_width // lanes) + more
+
+    def round_parts(slot, h):
+        return [w_out.at[round_piece(far_dp * depth, slot, h)]]
+
+    round_start, round_near_own, round_hop, round_near = gather(
+        round_parts, round_send, round_recv, round_swap_send, round_swap_recv
+    )
+    rounds = list(range(last + 1))
+    tasks = [key_near_own, functools.partial(attend, [0], True)]
     for j in range(last + 1):
         key_hop(j)
+        while j >= 3 and rounds and rounds[0] < min(last, 2 * j - 4):
+            round_hop(rounds.pop(0))
         for task in tasks:
             task()
         tasks = [functools.partial(key_near, j)]
-        if j == 3:
-            loads[3].wait()
+        if j == 0:
+            for h in (0, 1):
+                piece = w_out.at[round_piece(far_dp * depth, me, h)]
+                across(piece, piece, pieces + 1 + h).wait_recv()
+                round_start(h)
+        if j == 1:
+            loads[8].wait()
+            parted_hidden[...] = jnp.dot(split, hidden[...], preferred_element_type=f32).astype(bf16)
+        if j == last - 2:
+            loads[7].wait()
             pass_far(0)
+        if j == last - 1:
+            pass_far(1)
         if j % 2 == 1 or j == last:
             dist = step_of(0, j)[0]
             ks = [half_ring] if j == last else [dist, chips - dist]
-            tasks += [functools.partial(score_chip, k) for k in ks]
+            tasks.append(functools.partial(attend, ks))
     for task in tasks:
         task()
-    pass_far(1)
-
-    scale = score_scale * 1.4426950408889634
-    block = 64
-
-    for s in range(seqs):
-        top[s, :, pl.ds(0, 1)] = jnp.max(top[s], axis=1, keepdims=True)
-
-        def soften(i, carry, s=s):
-            part = pl.ds(pl.multiple_of(i * block, block), block)
-            shifted = (scores[s, part] - top[s, part, pl.ds(0, 1)]) * scale
-            weight = jnp.exp2(shifted)
-            probs[part] = weight.astype(bf16)
-            top[s, part, pl.ds(0, 1)] = 1.0 / jnp.sum(weight, axis=1, keepdims=True)
-            return carry
-
-        lax.fori_loop(0, row_count // block, soften, 0)
-        blend = jnp.dot(probs[...], keys[s], preferred_element_type=f32)
-        attended[s] = (blend * top[s, :, pl.ds(0, 1)]).astype(bf16)
-        if s == 0:
-            pass_far(2)
+    for i in rounds:
+        round_hop(i)
+
+    def row_parts(slot, h):
+        return [rows.at[slot, pl.ds(h * span_len + i * sub, sub)] for i in (0, 1)]
+
+    row_start, row_near_own, row_hop, row_near = gather(row_parts, row_send, row_recv, row_swap_send, row_swap_recv)
     await_near(0)
-    for h in range(head_count):
-        part = pl.ds(h * span_len, span_len)
-        both = jnp.concatenate([attended[0, part], attended[1, part]], axis=0)
-        values[:, pl.ds(h * value_dim, value_dim)] = jnp.dot(
-            both, w_uv[h], preferred_element_type=f32
-        ).astype(bf16)
-    woven = jnp.dot(weave, values[...], preferred_element_type=f32).astype(bf16)
-    values[...] = woven
-    loads[4].wait()
-    loads[5].wait()
-    depth = here * value_dim
     near_cols = pl.ds(pl.multiple_of(own_dp * depth, depth), depth)
     far_cols = pl.ds(pl.multiple_of(far_dp * depth, depth), depth)
-    kept[...] = hidden[...].astype(f32) + jnp.dot(values[:, near_cols], w_out[near_cols], preferred_element_type=f32)
-    for i in range(3, pieces + 1):
-        pass_far(i)
-    for i in range(1, pieces + 1):
-        await_near(i)
-    residual = kept[...] + jnp.dot(values[:, far_cols], w_out[far_cols], preferred_element_type=f32)
-    kept[...] = residual
-    mean_square = jnp.mean(residual * residual, axis=1, keepdims=True)
-    rows[me] = (residual * lax.rsqrt(mean_square + norm_eps) * gain_ref[...].astype(f32)).astype(bf16)
-
-    def row_parts(slot, h):
-        return [rows.at[slot, spans[h]]]
-
-    row_start, row_near_own, row_hop, row_near = gather(row_parts, row_send, row_recv, row_swap_send, row_swap_recv)
-    row_start()
-
-    hits, gates = [], []
+    loads[9].wait()
+    for s in range(seqs):
+        total = jnp.sum(mass[s], axis=1, keepdims=True)
+        attended[...] = (blend[s] / total).astype(bf16)
+        for h in range(head_count):
+            values[spans[s], pl.ds(h * value_dim, value_dim)] = jnp.dot(
+                attended[pl.ds(h * span_len, span_len)], w_uv[h], preferred_element_type=f32
+            ).astype(bf16)
+        residual = parted_hidden[spans[s]].astype(f32) + jnp.dot(
+            values[spans[s], near_cols], w_out[near_cols], preferred_element_type=f32
+        )
+        if s == 0:
+            for i in range(2, pieces + 1):
+                pass_far(i)
+            round_near_own()
+            for i in range(last + 1):
+                round_near(i)
+            for i in range(1, pieces + 1):
+                await_near(i)
+        residual = residual + jnp.dot(values[spans[s], far_cols], w_out[far_cols], preferred_element_type=f32)
+        mean_square = jnp.mean(residual * residual, axis=1, keepdims=True)
+        normed = residual * lax.rsqrt(mean_square + norm_eps) * gain[...].astype(f32)
+        rows[me, spans[s]] = normed.astype(bf16)
+        row_start(s)
+
+    woven = jnp.dot(weave, values[...], preferred_element_type=f32).astype(bf16)
+    kept[...] = (
+        hidden[...].astype(f32)
+        + jnp.dot(woven[:, :depth], w_out[pl.ds(0, depth)], preferred_element_type=f32)
+        + jnp.dot(woven[:, depth:], w_out[pl.ds(depth, depth)], preferred_element_type=f32)
+    )
+    hits, scales = [], []
     own_id = me.astype(f32)
     for c in range(chips):
         pair = jnp.concatenate([tables[2 * c], tables[2 * c + 1]], axis=1).astype(f32)
         matches = pair[:8] == own_id
         hits.append(jnp.max(jnp.where(matches, 1.0, 0.0), axis=0, keepdims=True))
-        gates.append(jnp.sum(jnp.where(matches, pair[8:], 0.0), axis=0, keepdims=True))
+        scales.append(jnp.sum(jnp.where(matches, pair[8:], 0.0), axis=0, keepdims=True))
     hits = jnp.concatenate(hits, axis=0)
     to = lax.broadcasted_iota(jnp.int32, (2 * count, 2 * count), 0)
     at = lax.broadcasted_iota(jnp.int32, (2 * count, 2 * count), 1)
@@ -545,9 +598,10 @@
     for c in range(chips):
         chosen = slot_id == ranks[c : c + 1]
         place[c] = jnp.where(chosen, 1.0, 0.0).astype(bf16)
-        weighed = jnp.where(chosen, gates[c], 0.0).astype(bf16)
-        mix[2 * c] = weighed[:, :count]
-        mix[2 * c + 1] = weighed[:, count:]
+        weighed = jnp.where(chosen, scales[c], 0.0).astype(bf16)
+        for i in (0, 1):
+            own_part = weighed[:, i * count : (i + 1) * count]
+            mix[2 * c + i] = jnp.dot(own_part, split, preferred_element_type=f32).astype(bf16)
 
     def start_experts(ks):
         picked = []
@@ -604,7 +658,7 @@
             ))
 
     row_near_own()
-    for load in loads[6:]:
+    for load in loads[10:]:
         load.wait()
     start_experts([0])
     end_experts([0])
@@ -630,6 +684,7 @@
     advance(1, 0)
 
     bring(0)
+    stores = []
     for h in (0, 1):
         total = mine[0, spans[h]].astype(f32) + paired[0, spans[h]].astype(f32)
         for way in (0, 1):
@@ -637,15 +692,18 @@
             await_ring(way, j)
             total = total + arrived[way, j].astype(f32)
         produced[spans[h]] = (kept[spans[h]] + total).astype(bf16)
-    store = pltpu.make_async_copy(produced, out_hbm.reshape(count, width), load_sem.at[0])
-    store.start()
-    store.wait()
+        stores.append(
+            pltpu.make_async_copy(produced.at[spans[h]], out_hbm.reshape(count, width).at[spans[h]], load_sem.at[h])
+        )
+        stores[h].start()
+    for store in stores:
+        store.wait()
     for copy in waits:
         copy.wait_send()
 
 
 def fused_layer(
-    table, limits, gain, latents, queries, memory, hidden, w_uv, w_out, w_gate_t, w_up_t, w_down, n, slots, collective_id
+    ids, gates, lengths, gain, latents, queries, memory, hidden, w_uv, w_out, w_gate_t, w_up_t, w_down, n, slots, collective_id
 ):
     span_len, seqs, width = hidden.shape
     count = span_len * seqs
@@ -660,24 +718,30 @@
     bf16, f32 = jnp.bfloat16, jnp.float32
     dma, vmem = pltpu.SemaphoreType.DMA, pltpu.VMEM
     row_count = head_count * span_len
-    pieces = 4
+    pieces = 2
     return pl.pallas_call(
         functools.partial(layer_kernel, n),
         out_shape=jax.ShapeDtypeStruct((span_len, seqs, width), bf16),
-        in_specs=[pl.BlockSpec(memory_space=pltpu.VMEM)] * 3 + [pl.BlockSpec(memory_space=pl.ANY)] * 9,
+        in_specs=[pl.BlockSpec(memory_space=pl.ANY)] * 13,
         out_specs=pl.BlockSpec(memory_space=pl.ANY),
         scratch_shapes=[
+            vmem(ids.shape, jnp.int32),
+            vmem(gates.shape, bf16),
+            vmem(lengths.shape, jnp.int32),
+            vmem(gain.shape, bf16),
             vmem((count, lat_width), bf16),
             vmem((count, head_count * lat_width), bf16),
             vmem((seqs * mem_len, lat_width), bf16),
             vmem((count, width), bf16),
+            vmem((count, width), bf16),
             vmem((seqs, key_total, lat_width), bf16),
             vmem((n, 16, count), bf16),
             vmem((seqs, row_count, lat_width), bf16),
-            vmem((seqs, row_count, key_total), f32),
-            vmem((row_count, key_total), bf16),
+            vmem((seqs, row_count, count), jnp.int32),
             vmem((seqs, row_count, count), f32),
-            vmem((seqs, row_count, lat_width), bf16),
+            vmem((seqs, row_count, count), f32),
+            vmem((seqs, row_count, lat_width), f32),
+            vmem((row_count, lat_width), bf16),
             vmem((count, head_count * value_dim), bf16),
             vmem((head_count, lat_width, value_dim), bf16),
             vmem((head_count * value_dim, width), bf16),
@@ -694,11 +758,15 @@
             vmem((chips, count, width), bf16),
             vmem((2, steps, count // 2, width), bf16),
             vmem((count, width), bf16),
-            dma((9,)),
+            dma((13,)),
+            dma((pieces + 3,)),
+            dma((pieces + 3,)),
             dma((pieces + 1,)),
             dma((pieces + 1,)),
-            dma((pieces + 1,)),
-            dma((pieces + 1,)),
+            dma((3, 2, steps)),
+            dma((3, 2, steps)),
+            dma((3, 2 * steps + 2)),
+            dma((3, 2 * steps + 2)),
             dma((2, 2, steps)),
             dma((2, 2, steps)),
             dma((2, 2 * steps + 2)),
@@ -719,15 +787,19 @@
             flops=6 * chips * slots * width * inner, bytes_accessed=32 * n * count * width, transcendentals=0
         ),
         name="layer_%d" % collective_id,
-    )(table, limits, gain, latents, queries, memory, hidden, w_uv, w_out, w_gate_t, w_up_t, w_down)
+    )(ids, gates, lengths, gain, latents, queries, memory, hidden, w_uv, w_out, w_gate_t, w_up_t, w_down)
+
+
+def round_share(depth, n):
+    return depth // (32 * n) * 16
 
 
 def layer_bytes(n, count, width, inner, slots, lat_width, head_count, value_dim):
     chips = n // 2
     key_total = (n + 2) * count // 2
     row_count = head_count * count // 2
-    front = count * (1 + head_count) * lat_width + 2 * key_total * lat_width + 4 * row_count * lat_width
-    front += 5 * row_count * key_total + 4 * row_count * count + head_count * value_dim * (lat_width + width + count)
+    front = count * (1 + head_count) * lat_width + 2 * key_total * lat_width + 3 * row_count * lat_width
+    front += 4 * row_count * lat_width + 12 * row_count * count + head_count * value_dim * (lat_width + width + count)
     back = n * count * width + 3 * width * inner + (4 * chips - 1) * count * width + 5 * count * width
     back += 4 * chips * slots * count + 2 * slots * inner
     return 2 * (front + back) + 8 * slots * inner * 2
@@ -772,17 +844,14 @@
         and seq_count == 2
         and row_count % 128 == 0
         and heads_here % 2 == 0
+        and heads_here * value_dim % (32 * n) == 0
         and mem_latents.shape[1] <= row_count
         and layer_bytes(n, row_count, model_width, w_down.shape[1], slots, latent_dim, head_count, value_dim)
         < 60 * 1024 * 1024
     )
     if fits:
-        pad = ((0, 8 - top_count), (0, 0))
-        table = jnp.concatenate(
-            [jnp.pad(ids_t, pad, constant_values=255), jnp.pad(gates_t, pad)], axis=0
-        )
         out = fused_layer(
-            table, jnp.broadcast_to(lengths[0][:, None], (seq_count, row_count)), norm_gain[None],
+            jnp.transpose(ids[0], (2, 1, 0)), jnp.transpose(gates[0], (2, 1, 0)), lengths, norm_gain,
             latents[0], queries[0], mem_latents[0], hidden[0], w_uv, w_out,
             jnp.transpose(w_gate[0]), jnp.transpose(w_up[0]), w_down[0], n, slots, 4,
         )

time: 135 us -> 122 us (0.904)
  Pallas kernels: 127 us -> 120 us
  local copies, waits for them, and re-layouts: 5.61 us -> 2.2 us
    pallas_call x1, Pallas kernels: 127 us -> 120 us  [fused_layer(): pl.pallas_call(functools.partial(layer_kernel, n), out_shape=jax.ShapeDty...]
    broadcast_in_dim x2 -> x0, local copies, waits for them, and re-layouts: 2.56 us -> none  [the longest x1 1.29 us: shards(): norm_gain[None]]
where the time goes in v3:
time: 122 us
  Pallas kernels  120 us (98%)
  local copies, waits for them, and re-layouts  2.2 us (2%)
    pallas_call x1, Pallas kernels, fused_layer(): pl.pallas_call(functools.partial(layer_kernel, n), out_shape=jax.ShapeDty...  120 us

profile of v3, /device:TPU:0, one launch (start us, length us, event | category | flops | bytes accessed | tf_op | source)
XLA Modules:
  0.0 121.7 jit_solution(4346938514429708888)
XLA Ops:
  0.0 119.5 %layer_4.1 = bf16[64,2,2048]{2,1,0:T(2,128)(2,1)} custom-call(s32[6,2,64]{2,1,0:T(2,128)} %bitcast.26, bf16[6,2,64]{2,1,0:T(2,128)(2,1)} %bitcast.27, s32[1,2]{1,0:T(1,128)} %limit_hbm.1, bf16[2048]{0:T(1024)(128)(2,1)} %gain_hbm.1, bf16[64,2,512]{2,1,0:T(2,128)(2,1)} %bitcast.24, bf16[64,2,4096]{2,1,0:T(2,128)(2,1)} %bitcast.22, ...), custom_call_target="tpu_custom_call" | custom-call | flops 8858370048 | bytes 134217728 | tf_op jit(solution)/shard_map/layer_4/pallas_call | solution.py:722
  119.6 2.2 %copy.15 = bf16[1,64,2,2048]{3,2,1,0:T(2,128)(2,1)} copy(bf16[1,64,2,2048]{3,2,1,0:T(2,128)(2,1)} %bitcast.18) | data formatting | bytes 1048576

commit v4 on v3

--- a/solution.py
+++ b/solution.py
@@ -266,11 +266,11 @@
     n,
     ids_hbm, gates_hbm, limit_hbm, gain_hbm,
     latent_hbm, query_hbm, memory_hbm, hidden_hbm, uv_hbm, wout_hbm, gate_hbm, up_hbm, down_hbm,
-    out_hbm,
+    out_ref,
     ids, gates, limit, gain,
     latent, query, memory, hidden, parted_hidden, keys, tables, heads, bound, peak, mass, blend,
     attended, values, w_uv, w_out, kept,
-    place, mix, rows, w_gate, w_up, w_down, act, mine, paired, give, arrived, produced,
+    place, mix, rows, w_gate, w_up, w_down, act, mine, paired, give, arrived,
     load_sem, far_send, far_recv, near_send, near_recv,
     key_send, key_recv, key_swap_send, key_swap_recv,
     row_send, row_recv, row_swap_send, row_swap_recv,
@@ -345,8 +345,8 @@
         return pl.ds(pl.multiple_of(at, 8), out_rows)
 
     def round_piece(first, slot, h):
-        size = round_rows // 2
-        return pl.ds(pl.multiple_of(first + slot * round_rows + h * size, 8), size)
+        size = -(-round_rows // 16) * 8
+        return pl.ds(pl.multiple_of(first + slot * round_rows + h * size, 8), size if h == 0 else round_rows - size)
 
     def across(src, dst, i):
         return pltpu.make_async_remote_copy(
@@ -433,11 +433,14 @@
 
     sub = span_len // 2
 
-    def key_parts(slot, h):
-        found = [keys.at[h, place_of(slot, i * sub, sub)] for i in (0, 1)]
-        return found + ([tables.at[slot]] if h == 0 else [])
-
-    key_start, key_near_own, key_hop, key_near = gather(key_parts, key_send, key_recv, key_swap_send, key_swap_recv)
+    def key_parts(s):
+        def parts(slot, h):
+            found = [keys.at[s, place_of(slot, h * sub, sub)]]
+            return found + ([tables.at[slot]] if s == 0 and h == 0 else [])
+
+        return gather(parts, key_send.at[s], key_recv.at[s], key_swap_send.at[s], key_swap_recv.at[s])
+
+    streams = [key_parts(s) for s in range(seqs)]
     for load in loads[:5]:
         load.wait()
     lines = []
@@ -451,7 +454,8 @@
         keys[s, place_of(me, 0, span_len)] = jnp.dot(
             split[s * span_len : (s + 1) * span_len], latent[...], preferred_element_type=f32
         ).astype(bf16)
-        key_start(s)
+        for h in (0, 1):
+            streams[s][0](h)
 
     loads[5].wait()
     for s in range(seqs):
@@ -478,9 +482,9 @@
     def wide(x, times):
         return x if times == 1 else jnp.concatenate([x] * times, axis=1)
 
-    def attend(ks, opening=False):
+    def attend(ks, chosen_seqs, opening=False):
         firsts = [pl.multiple_of(device(k, 0) * span_len, lanes) for k in ks]
-        for s in range(seqs):
+        for s in chosen_seqs:
             held = [keys[s, pl.ds(first, lanes)] for first in firsts]
             seen_keys = [first <= bound[s] for first in firsts]
             if opening:
@@ -512,36 +516,49 @@
     round_start, round_near_own, round_hop, round_near = gather(
         round_parts, round_send, round_recv, round_swap_send, round_swap_recv
     )
-    rounds = list(range(last + 1))
-    tasks = [key_near_own, functools.partial(attend, [0], True)]
-    for j in range(last + 1):
-        key_hop(j)
-        while j >= 3 and rounds and rounds[0] < min(last, 2 * j - 4):
-            round_hop(rounds.pop(0))
-        for task in tasks:
-            task()
-        tasks = [functools.partial(key_near, j)]
-        if j == 0:
+    def steps_at(dist):
+        return (last,) if dist == half_ring else (2 * dist - 2, 2 * dist - 1)
+
+    def at_dist(dist):
+        return [half_ring] if dist == half_ring else [dist, chips - dist]
+
+    def hop_all(stream, dist):
+        for j in steps_at(dist):
+            stream[2](j)
+
+    def use_keys(chosen_seqs, dist):
+        for s in chosen_seqs:
+            for j in steps_at(dist):
+                streams[s][3](j)
+        attend(at_dist(dist), chosen_seqs)
+
+    rounds = (round_start, round_near_own, round_hop, round_near)
+    for dist in range(1, half_ring):
+        for s in range(seqs):
+            hop_all(streams[s], dist)
+        if dist == 1:
             for h in (0, 1):
                 piece = w_out.at[round_piece(far_dp * depth, me, h)]
                 across(piece, piece, pieces + 1 + h).wait_recv()
                 round_start(h)
-        if j == 1:
+            for s in range(seqs):
+                streams[s][1]()
+            attend([0], range(seqs), True)
             loads[8].wait()
             parted_hidden[...] = jnp.dot(split, hidden[...], preferred_element_type=f32).astype(bf16)
-        if j == last - 2:
-            loads[7].wait()
-            pass_far(0)
-        if j == last - 1:
-            pass_far(1)
-        if j % 2 == 1 or j == last:
-            dist = step_of(0, j)[0]
-            ks = [half_ring] if j == last else [dist, chips - dist]
-            tasks.append(functools.partial(attend, ks))
-    for task in tasks:
-        task()
-    for i in rounds:
-        round_hop(i)
+        else:
+            hop_all(rounds, dist - 1)
+            use_keys(range(seqs), dist - 1)
+    loads[7].wait()
+    pass_far(0)
+    for s in range(seqs):
+        hop_all(streams[s], half_ring)
+    pass_far(1)
+    hop_all(rounds, half_ring - 1)
+    use_keys(range(seqs), half_ring - 1)
+    use_keys([0], half_ring)
+    for i in range(2, pieces + 1):
+        pass_far(i)
 
     def row_parts(slot, h):
         return [rows.at[slot, pl.ds(h * span_len + i * sub, sub)] for i in (0, 1)]
@@ -552,6 +569,8 @@
     far_cols = pl.ds(pl.multiple_of(far_dp * depth, depth), depth)
     loads[9].wait()
     for s in range(seqs):
+        if s == 1:
+            use_keys([1], half_ring)
         total = jnp.sum(mass[s], axis=1, keepdims=True)
         attended[...] = (blend[s] / total).astype(bf16)
         for h in range(head_count):
@@ -562,8 +581,7 @@
             values[spans[s], near_cols], w_out[near_cols], preferred_element_type=f32
         )
         if s == 0:
-            for i in range(2, pieces + 1):
-                pass_far(i)
+            hop_all(rounds, half_ring)
             round_near_own()
             for i in range(last + 1):
                 round_near(i)
@@ -636,26 +654,28 @@
     def index_of(dist, h):
         return 0 if dist == half_ring else 1 + 2 * (half_ring - 1 - dist) + h
 
-    def await_ring(way, j):
-        piece = arrived.at[way, j]
-        remote(piece, piece, ring_send.at[way, j], ring_recv.at[way, j], ahead[way]).wait_recv()
+    def await_ring(way, j, u):
+        piece = arrived.at[way, j, pl.ds(u * sub, sub)]
+        remote(piece, piece, ring_send.at[u, way, j], ring_recv.at[u, way, j], ahead[way]).wait_recv()
 
     def advance(dist, chain):
-        for way in (0, 1):
-            h = way if chain == 0 else 1 - way
-            k = offset(way, dist)
-            bring(k)
-            total = mine[k, spans[h]].astype(f32) + paired[k, spans[h]].astype(f32)
-            if dist < half_ring - chain:
-                j = index_of(dist + 1, h)
-                await_ring(way, j)
-                total = total + arrived[way, j].astype(f32)
-            mine[k, spans[h]] = total.astype(bf16)
-            j = index_of(dist, h)
-            send(remote(
-                mine.at[k, spans[h]], arrived.at[way, j],
-                ring_send.at[way, j], ring_recv.at[way, j], ahead[way],
-            ))
+        for u in (0, 1):
+            for way in (0, 1):
+                h = way if chain == 0 else 1 - way
+                k = offset(way, dist)
+                bring(k)
+                part, within = pl.ds(h * span_len + u * sub, sub), pl.ds(u * sub, sub)
+                total = mine[k, part].astype(f32) + paired[k, part].astype(f32)
+                if dist < half_ring - chain:
+                    j = index_of(dist + 1, h)
+                    await_ring(way, j, u)
+                    total = total + arrived[way, j, within].astype(f32)
+                mine[k, part] = total.astype(bf16)
+                j = index_of(dist, h)
+                send(remote(
+                    mine.at[k, part], arrived.at[way, j, within],
+                    ring_send.at[u, way, j], ring_recv.at[u, way, j], ahead[way],
+                ))
 
     row_near_own()
     for load in loads[10:]:
@@ -665,7 +685,8 @@
 
     tasks = []
     for j in range(last + 1):
-        row_hop(j)
+        if j < last:
+            row_hop(j)
         if j % 2 == 1 or j == last:
             for i in (j - 1, j) if j % 2 == 1 else (j,):
                 row_near(i)
@@ -675,6 +696,7 @@
         for _ in range(min(len(tasks), 1 if j < last - 1 else len(tasks))):
             tasks.pop(0)()
         if j == last - 1:
+            row_hop(last)
             advance(half_ring - 1, 1)
 
     advance(half_ring, 0)
@@ -684,20 +706,14 @@
     advance(1, 0)
 
     bring(0)
-    stores = []
-    for h in (0, 1):
-        total = mine[0, spans[h]].astype(f32) + paired[0, spans[h]].astype(f32)
+    for u, h in ((0, 0), (0, 1), (1, 0), (1, 1)):
+        part, within = pl.ds(h * span_len + u * sub, sub), pl.ds(u * sub, sub)
+        total = kept[part] + mine[0, part].astype(f32) + paired[0, part].astype(f32)
         for way in (0, 1):
             j = index_of(1, h)
-            await_ring(way, j)
-            total = total + arrived[way, j].astype(f32)
-        produced[spans[h]] = (kept[spans[h]] + total).astype(bf16)
-        stores.append(
-            pltpu.make_async_copy(produced.at[spans[h]], out_hbm.reshape(count, width).at[spans[h]], load_sem.at[h])
-        )
-        stores[h].start()
-    for store in stores:
-        store.wait()
+            await_ring(way, j, u)
+            total = total + arrived[way, j, within].astype(f32)
+        out_ref[part] = total.astype(bf16)
     for copy in waits:
         copy.wait_send()
 
@@ -721,9 +737,9 @@
     pieces = 2
     return pl.pallas_call(
         functools.partial(layer_kernel, n),
-        out_shape=jax.ShapeDtypeStruct((span_len, seqs, width), bf16),
+        out_shape=pltpu.VMEM((count, width), bf16),
         in_specs=[pl.BlockSpec(memory_space=pl.ANY)] * 13,
-        out_specs=pl.BlockSpec(memory_space=pl.ANY),
+        out_specs=pl.BlockSpec(memory_space=pltpu.VMEM),
         scratch_shapes=[
             vmem(ids.shape, jnp.int32),
             vmem(gates.shape, bf16),
@@ -757,16 +773,15 @@
             vmem((chips, count, width), bf16),
             vmem((chips, count, width), bf16),
             vmem((2, steps, count // 2, width), bf16),
-            vmem((count, width), bf16),
             dma((13,)),
             dma((pieces + 3,)),
             dma((pieces + 3,)),
             dma((pieces + 1,)),
             dma((pieces + 1,)),
-            dma((3, 2, steps)),
-            dma((3, 2, steps)),
-            dma((3, 2 * steps + 2)),
-            dma((3, 2 * steps + 2)),
+            dma((2, 2, 2, steps)),
+            dma((2, 2, 2, steps)),
+            dma((2, 2, 2 * steps + 2)),
+            dma((2, 2, 2 * steps + 2)),
             dma((2, 2, steps)),
             dma((2, 2, steps)),
             dma((2, 2 * steps + 2)),
@@ -775,13 +790,13 @@
             dma((1, 2, steps)),
             dma((1, 2 * steps + 2)),
             dma((1, 2 * steps + 2)),
-            dma((2, steps)),
-            dma((2, steps)),
+            dma((2, 2, steps)),
+            dma((2, 2, steps)),
             dma((chips,)),
             dma((chips,)),
         ],
         compiler_params=pltpu.CompilerParams(
-            collective_id=collective_id, has_side_effects=True, vmem_limit_bytes=67000000
+            collective_id=collective_id, has_side_effects=True, vmem_limit_bytes=61000000
         ),
         cost_estimate=pl.CostEstimate(
             flops=6 * chips * slots * width * inner, bytes_accessed=32 * n * count * width, transcendentals=0
@@ -791,7 +806,7 @@
 
 
 def round_share(depth, n):
-    return depth // (32 * n) * 16
+    return depth // (2 * n) // 16 * 16
 
 
 def layer_bytes(n, count, width, inner, slots, lat_width, head_count, value_dim):
@@ -844,7 +859,8 @@
         and seq_count == 2
         and row_count % 128 == 0
         and heads_here % 2 == 0
-        and heads_here * value_dim % (32 * n) == 0
+        and heads_here * value_dim % (64 * n // 4) == 0
+        and round_share(heads_here * value_dim, n) >= 16
         and mem_latents.shape[1] <= row_count
         and layer_bytes(n, row_count, model_width, w_down.shape[1], slots, latent_dim, head_count, value_dim)
         < 60 * 1024 * 1024
@@ -855,7 +871,7 @@
             latents[0], queries[0], mem_latents[0], hidden[0], w_uv, w_out,
             jnp.transpose(w_gate[0]), jnp.transpose(w_up[0]), w_down[0], n, slots, 4,
         )
-        return out[None]
+        return out.reshape(1, local_len, seq_count, model_width)
 
     half_heads = heads_here // 2
     uv_half = lax.dynamic_slice_in_dim(w_uv, core * half_heads, half_heads, 0)

time: 122 us -> 117 us (0.959)
  Pallas kernels: 120 us -> 116 us
    pallas_call x1, Pallas kernels: 120 us -> 116 us  [fused_layer(): pl.pallas_call(functools.partial(layer_kernel, n), out_shape=pltpu.VMEM((...]
    unnamed x1 -> x0, local copies, waits for them, and re-layouts: 2.2 us -> none
where the time goes in v4:
time: 117 us
  Pallas kernels  116 us (99%)
    pallas_call x1, Pallas kernels, fused_layer(): pl.pallas_call(functools.partial(layer_kernel, n), out_shape=pltpu.VMEM((...  116 us

profile of v4, /device:TPU:0, one launch (start us, length us, event | category | flops | bytes accessed | tf_op | source)
XLA Modules:
  0.0 117.3 jit_solution(16392238300836462089)
XLA Ops:
  0.0 116.1 %layer_4.1 = bf16[128,2048]{1,0:T(8,128)(2,1)S(1)} custom-call(s32[6,2,64]{2,1,0:T(2,128)} %bitcast.24, bf16[6,2,64]{2,1,0:T(2,128)(2,1)} %bitcast.25, s32[1,2]{1,0:T(1,128)} %limit_hbm.1, bf16[2048]{0:T(1024)(128)(2,1)} %gain_hbm.1, bf16[64,2,512]{2,1,0:T(2,128)(2,1)} %bitcast.22, bf16[64,2,4096]{2,1,0:T(2,128)(2,1)} %bitcast.20, ...), custom_call_target="tpu_custom_call" | custom-call | flops 8858370048 | bytes 134217728 | tf_op jit(solution)/shard_map/layer_4/pallas_call | solution.py:738
  116.1 1.1 reshape.3

commit v5 on v4

--- a/solution.py
+++ b/solution.py
@@ -308,11 +308,11 @@
             (gates_hbm, gates),
             (limit_hbm, limit),
             (gain_hbm, gain),
+            (wout_hbm, w_out.at[pl.ds(own_dp * here * value_dim, here * value_dim)]),
+            (uv_hbm, w_uv.at[pl.ds(own_dp * here, here)]),
             (query_hbm.reshape(query.shape), query),
             (memory_hbm.reshape(memory.shape), memory),
-            (uv_hbm, w_uv.at[pl.ds(own_dp * here, here)]),
             (hidden_hbm.reshape(count, width), hidden),
-            (wout_hbm, w_out.at[pl.ds(own_dp * here * value_dim, here * value_dim)]),
             (gate_hbm, w_gate),
             (up_hbm, w_up),
             (down_hbm, w_down),
@@ -330,8 +330,6 @@
     for target in (ahead[0], ahead[1], partner):
         pl.semaphore_signal(barrier, inc=1, device_id={"expert": target}, device_id_type=MESH)
     pl.semaphore_signal(barrier, inc=1, device_id={"dp": far_dp}, device_id_type=MESH)
-    pl.semaphore_wait(barrier, 4)
-
     def uv_piece(owner, of_core):
         return pl.ds(owner * here + of_core * half_here, half_here)
 
@@ -353,12 +351,6 @@
             src_ref=src, dst_ref=dst, send_sem=far_send.at[i], recv_sem=far_recv.at[i],
             device_id={"dp": far_dp}, device_id_type=MESH,
         )
-
-    for h in (0, 1):
-        send(across(wout_hbm.at[round_piece(0, me, h)], w_out.at[round_piece(own_dp * depth, me, h)], pieces + 1 + h))
-    send(across(uv_hbm.at[pl.ds(core * half_here, half_here)], w_uv.at[uv_piece(own_dp, core)], 0))
-    for i in range(pieces):
-        send(across(wout_hbm.at[out_piece(0, core, i)], w_out.at[out_piece(own_dp * depth, core, i)], i + 1))
 
     def far_ref(i, of_core):
         return w_uv.at[uv_piece(far_dp, of_core)] if i == 0 else w_out.at[out_piece(far_dp * depth, of_core, i - 1)]
@@ -399,15 +391,17 @@
                 onward = [last if j == last - 2 + way else None for way in (0, 1)]
             if j == last:
                 onward = [None, None]
+            found = []
             for way in (0, 1):
                 dist, h = step_of(way, j)
-                for i, ref in enumerate(parts(device(-dist if way == 0 else dist, core), h)):
-                    remote(ref, ref, sends.at[i, way, j], recvs.at[i, way, j], ahead[way]).wait_recv()
-                    if onward[way] is not None:
-                        k = onward[way]
-                        send(remote(ref, ref, sends.at[i, way, k], recvs.at[i, way, k], ahead[way]))
-                    k = 2 * j + way
-                    send(remote(ref, ref, swap_sends.at[i, k], swap_recvs.at[i, k], partner))
+                found += [(i, way, ref) for i, ref in enumerate(parts(device(-dist if way == 0 else dist, core), h))]
+            for i, way, ref in sorted(found, key=lambda piece: piece[:2]):
+                remote(ref, ref, sends.at[i, way, j], recvs.at[i, way, j], ahead[way]).wait_recv()
+                if onward[way] is not None:
+                    k = onward[way]
+                    send(remote(ref, ref, sends.at[i, way, k], recvs.at[i, way, k], ahead[way]))
+                k = 2 * j + way
+                send(remote(ref, ref, swap_sends.at[i, k], swap_recvs.at[i, k], partner))
 
         def near(j):
             for way in (0, 1):
@@ -454,17 +448,29 @@
         keys[s, place_of(me, 0, span_len)] = jnp.dot(
             split[s * span_len : (s + 1) * span_len], latent[...], preferred_element_type=f32
         ).astype(bf16)
+    pl.semaphore_wait(barrier, 4)
+    loads[5].wait()
+    for h in (0, 1):
+        piece = w_out.at[round_piece(own_dp * depth, me, h)]
+        send(across(piece, piece, pieces + 1 + h))
+    loads[6].wait()
+    piece = w_uv.at[uv_piece(own_dp, core)]
+    send(across(piece, piece, 0))
+    for i in range(pieces):
+        piece = w_out.at[out_piece(own_dp * depth, core, i)]
+        send(across(piece, piece, i + 1))
+    for s in range(seqs):
         for h in (0, 1):
             streams[s][0](h)
 
-    loads[5].wait()
+    loads[7].wait()
     for s in range(seqs):
         parted = jnp.dot(
             split[s * span_len : (s + 1) * span_len], query[...], preferred_element_type=f32
         ).astype(bf16)
         for h in range(head_count):
             heads[s, pl.ds(h * span_len, span_len)] = parted[:, h * lat_width : (h + 1) * lat_width]
-    loads[6].wait()
+    loads[8].wait()
     parted = jnp.dot(split_of(2 * mem_len), memory[...], preferred_element_type=f32).astype(bf16)
     lanes = 2 * span_len
     row_count = head_count * span_len
@@ -533,29 +539,30 @@
         attend(at_dist(dist), chosen_seqs)
 
     rounds = (round_start, round_near_own, round_hop, round_near)
+    for h in (0, 1):
+        piece = w_out.at[round_piece(far_dp * depth, me, h)]
+        across(piece, piece, pieces + 1 + h).wait_recv()
+        round_start(h)
     for dist in range(1, half_ring):
+        if dist > 1:
+            hop_all(rounds, dist - 1)
         for s in range(seqs):
             hop_all(streams[s], dist)
         if dist == 1:
-            for h in (0, 1):
-                piece = w_out.at[round_piece(far_dp * depth, me, h)]
-                across(piece, piece, pieces + 1 + h).wait_recv()
-                round_start(h)
             for s in range(seqs):
                 streams[s][1]()
             attend([0], range(seqs), True)
-            loads[8].wait()
+            loads[9].wait()
             parted_hidden[...] = jnp.dot(split, hidden[...], preferred_element_type=f32).astype(bf16)
         else:
-            hop_all(rounds, dist - 1)
             use_keys(range(seqs), dist - 1)
-    loads[7].wait()
     pass_far(0)
+    hop_all(rounds, half_ring - 1)
+    use_keys(range(seqs), half_ring - 1)
     for s in range(seqs):
         hop_all(streams[s], half_ring)
     pass_far(1)
-    hop_all(rounds, half_ring - 1)
-    use_keys(range(seqs), half_ring - 1)
+    hop_all(rounds, half_ring)
     use_keys([0], half_ring)
     for i in range(2, pieces + 1):
         pass_far(i)
@@ -567,7 +574,6 @@
     await_near(0)
     near_cols = pl.ds(pl.multiple_of(own_dp * depth, depth), depth)
     far_cols = pl.ds(pl.multiple_of(far_dp * depth, depth), depth)
-    loads[9].wait()
     for s in range(seqs):
         if s == 1:
             use_keys([1], half_ring)
@@ -581,7 +587,6 @@
             values[spans[s], near_cols], w_out[near_cols], preferred_element_type=f32
         )
         if s == 0:
-            hop_all(rounds, half_ring)
             round_near_own()
             for i in range(last + 1):
                 round_near(i)

time: 117 us -> 117 us (level)
  no operation moved by 1% of the time
where the time goes in v5:
time: 117 us
  Pallas kernels  116 us (99%)
    pallas_call x1, Pallas kernels, fused_layer(): pl.pallas_call(functools.partial(layer_kernel, n), out_shape=pltpu.VMEM((...  116 us

profile of v5, /device:TPU:0, one launch (start us, length us, event | category | flops | bytes accessed | tf_op | source)
XLA Modules:
  0.0 116.7 jit_solution(9661904733165689313)
XLA Ops:
  0.0 115.5 %layer_4.1 = bf16[128,2048]{1,0:T(8,128)(2,1)S(1)} custom-call(s32[6,2,64]{2,1,0:T(2,128)} %bitcast.24, bf16[6,2,64]{2,1,0:T(2,128)(2,1)} %bitcast.25, s32[1,2]{1,0:T(1,128)} %limit_hbm.1, bf16[2048]{0:T(1024)(128)(2,1)} %gain_hbm.1, bf16[64,2,512]{2,1,0:T(2,128)(2,1)} %bitcast.22, bf16[64,2,4096]{2,1,0:T(2,128)(2,1)} %bitcast.20, ...), custom_call_target="tpu_custom_call" | custom-call | flops 8858370048 | bytes 134217728 | tf_op jit(solution)/shard_map/layer_4/pallas_call | solution.py:743
  115.5 1.1 reshape.3

commit v6 on v5

--- a/solution.py
+++ b/solution.py
@@ -370,20 +370,20 @@
     def offset(way, dist):
         return dist if way == 0 else chips - dist
 
-    def gather(parts, sends, recvs, swap_sends, swap_recvs):
+    def gather(parts, sends, recvs, swap_sends, swap_recvs, base=0):
         own = 2 * last + 2
 
         def start(h):
             for way in (0, 1):
                 for i, ref in enumerate(parts(me, h)):
-                    send(remote(ref, ref, sends.at[i, way, h], recvs.at[i, way, h], ahead[way]))
+                    send(remote(ref, ref, sends.at[base + i, way, h], recvs.at[base + i, way, h], ahead[way]))
             for i, ref in enumerate(parts(me, h)):
-                send(remote(ref, ref, swap_sends.at[i, own + h], swap_recvs.at[i, own + h], partner))
+                send(remote(ref, ref, swap_sends.at[base + i, own + h], swap_recvs.at[base + i, own + h], partner))
 
         def near_own():
             for h in (0, 1):
                 for i, ref in enumerate(parts(partner, h)):
-                    remote(ref, ref, swap_sends.at[i, own + h], swap_recvs.at[i, own + h], partner).wait_recv()
+                    remote(ref, ref, swap_sends.at[base + i, own + h], swap_recvs.at[base + i, own + h], partner).wait_recv()
 
         def hop(j):
             onward = [j + 2, j + 2]
@@ -396,19 +396,19 @@
                 dist, h = step_of(way, j)
                 found += [(i, way, ref) for i, ref in enumerate(parts(device(-dist if way == 0 else dist, core), h))]
             for i, way, ref in sorted(found, key=lambda piece: piece[:2]):
-                remote(ref, ref, sends.at[i, way, j], recvs.at[i, way, j], ahead[way]).wait_recv()
+                remote(ref, ref, sends.at[base + i, way, j], recvs.at[base + i, way, j], ahead[way]).wait_recv()
                 if onward[way] is not None:
                     k = onward[way]
-                    send(remote(ref, ref, sends.at[i, way, k], recvs.at[i, way, k], ahead[way]))
+                    send(remote(ref, ref, sends.at[base + i, way, k], recvs.at[base + i, way, k], ahead[way]))
                 k = 2 * j + way
-                send(remote(ref, ref, swap_sends.at[i, k], swap_recvs.at[i, k], partner))
+                send(remote(ref, ref, swap_sends.at[base + i, k], swap_recvs.at[base + i, k], partner))
 
         def near(j):
             for way in (0, 1):
                 dist, h = step_of(way, j)
                 k = 2 * j + way
                 for i, ref in enumerate(parts(device(-dist if way == 0 else dist, 1 - core), h)):
-                    remote(ref, ref, swap_sends.at[i, k], swap_recvs.at[i, k], partner).wait_recv()
+                    remote(ref, ref, swap_sends.at[base + i, k], swap_recvs.at[base + i, k], partner).wait_recv()
 
         return start, near_own, hop, near
 
@@ -432,7 +432,7 @@
             found = [keys.at[s, place_of(slot, h * sub, sub)]]
             return found + ([tables.at[slot]] if s == 0 and h == 0 else [])
 
-        return gather(parts, key_send.at[s], key_recv.at[s], key_swap_send.at[s], key_swap_recv.at[s])
+        return gather(parts, key_send, key_recv, key_swap_send, key_swap_recv, 2 * s)
 
     streams = [key_parts(s) for s in range(seqs)]
     for load in loads[:5]:
@@ -783,10 +783,10 @@
             dma((pieces + 3,)),
             dma((pieces + 1,)),
             dma((pieces + 1,)),
-            dma((2, 2, 2, steps)),
-            dma((2, 2, 2, steps)),
-            dma((2, 2, 2 * steps + 2)),
-            dma((2, 2, 2 * steps + 2)),
+            dma((3, 2, steps)),
+            dma((3, 2, steps)),
+            dma((3, 2 * steps + 2)),
+            dma((3, 2 * steps + 2)),
             dma((2, 2, steps)),
             dma((2, 2, steps)),
             dma((2, 2 * steps + 2)),

time: 117 us -> 116 us (level)
  no operation moved by 1% of the time
where the time goes in v6:
time: 116 us
  Pallas kernels  115 us (99%)
    pallas_call x1, Pallas kernels, fused_layer(): pl.pallas_call(functools.partial(layer_kernel, n), out_shape=pltpu.VMEM((...  115 us

profile of v6, /device:TPU:0, one launch (start us, length us, event | category | flops | bytes accessed | tf_op | source)
XLA Modules:
  0.0 116.1 jit_solution(13655087098960980855)
XLA Ops:
  0.0 115.0 %layer_4.1 = bf16[128,2048]{1,0:T(8,128)(2,1)S(1)} custom-call(s32[6,2,64]{2,1,0:T(2,128)} %bitcast.24, bf16[6,2,64]{2,1,0:T(2,128)(2,1)} %bitcast.25, s32[1,2]{1,0:T(1,128)} %limit_hbm.1, bf16[2048]{0:T(1024)(128)(2,1)} %gain_hbm.1, bf16[64,2,512]{2,1,0:T(2,128)(2,1)} %bitcast.22, bf16[64,2,4096]{2,1,0:T(2,128)(2,1)} %bitcast.20, ...), custom_call_target="tpu_custom_call" | custom-call | flops 8858370048 | bytes 134217728 | tf_op jit(solution)/shard_map/layer_4/pallas_call | solution.py:743
  115.0 1.1 reshape.3
